TPU v7x, 128 devices: a whole 4x4x4 slice. The times are simulated.
128 devices in a mesh: z: 4 (over z), y: 4 (over y), x: 8 (over x, core).
Axes of the slice: x: 4, y: 4, z: 4, core: 2. Of those that a mesh axis runs over, the one named last changes fastest.
Arguments:
- acts_in: bfloat16 [262144, 512], P(('z', 'y', 'x'))
- grad_out: bfloat16 [262144, 512], P(('z', 'y', 'x'))
- w_up1: bfloat16 [512, 2048], replicated
- w_down1: bfloat16 [2048, 512], replicated
- w_up2: bfloat16 [512, 2048], replicated
- w_down2: bfloat16 [2048, 512], replicated
Outputs:
- output 1: float32 [512, 2048], replicated
- output 2: float32 [2048, 512], replicated
- output 3: float32 [512, 2048], replicated
- output 4: float32 [2048, 512], replicated
- output 5: bfloat16 [262144, 512], P(('z', 'y', 'x'))
All inputs are finite; a program needn't handle non-finite values.
Results may differ from a plain program's by a relative error of at most 0.0134572.
Values are sent between devices in bfloat16 or wider.
A program may use at most 1 GiB of HBM per device.

v0:
```python
import math
import jax
import jax.numpy as jnp
from jax import lax
from jax.sharding import PartitionSpec as P

INV_ROOT_TWO = 1.0 / math.sqrt(2.0)
INV_ROOT_TWO_PI = 1.0 / math.sqrt(2.0 * math.pi)
ROW_CONTRACT = (((0,), (0,)), ((), ()))
COL_CONTRACT = (((1,), (1,)), ((), ()))


def gelu_slope(pre_act):
    return 0.5 * (1.0 + lax.erf(pre_act * INV_ROOT_TWO)) + pre_act * jnp.exp(-0.5 * pre_act * pre_act) * INV_ROOT_TWO_PI


def matmul(lhs, rhs):
    return jnp.dot(lhs, rhs, preferred_element_type=jnp.float32)


def contract(lhs, rhs, dims):
    return lax.dot_general(lhs, rhs, dims, preferred_element_type=jnp.float32)


def local_backward(acts_local, grad_top, w_up1, w_down1, w_up2, w_down2, reduce_fn):
    pre_one = matmul(acts_local, w_up1).astype(jnp.bfloat16)
    hid_one = jax.nn.gelu(pre_one.astype(jnp.float32), approximate=False).astype(jnp.bfloat16)
    mid_res = (matmul(hid_one, w_down1) + acts_local.astype(jnp.float32)).astype(jnp.bfloat16)
    pre_two = matmul(mid_res, w_up2).astype(jnp.bfloat16)
    hid_two = jax.nn.gelu(pre_two.astype(jnp.float32), approximate=False).astype(jnp.bfloat16)
    gw_down2 = reduce_fn(contract(hid_two, grad_top, ROW_CONTRACT))
    grad_hid2 = contract(grad_top, w_down2, COL_CONTRACT).astype(jnp.bfloat16)
    grad_pre2 = (grad_hid2.astype(jnp.float32) * gelu_slope(pre_two.astype(jnp.float32))).astype(jnp.bfloat16)
    gw_up2 = reduce_fn(contract(mid_res, grad_pre2, ROW_CONTRACT))
    grad_mid = (contract(grad_pre2, w_up2, COL_CONTRACT) + grad_top.astype(jnp.float32)).astype(jnp.bfloat16)
    gw_down1 = reduce_fn(contract(hid_one, grad_mid, ROW_CONTRACT))
    grad_hid1 = contract(grad_mid, w_down1, COL_CONTRACT).astype(jnp.bfloat16)
    grad_pre1 = (grad_hid1.astype(jnp.float32) * gelu_slope(pre_one.astype(jnp.float32))).astype(jnp.bfloat16)
    gw_up1 = reduce_fn(contract(acts_local, grad_pre1, ROW_CONTRACT))
    grad_acts = (contract(grad_pre1, w_up1, COL_CONTRACT) + grad_mid.astype(jnp.float32)).astype(jnp.bfloat16)
    return (gw_up1, gw_down1, gw_up2, gw_down2, grad_acts)


def solution(mesh):
    n_dev = math.prod(mesh.shape.values())
    batch_spec = P(('z', 'y', 'x'), None)
    full_spec = P(None, None)

    def reduce_grad(local_grad):
        grad_piece = lax.psum_scatter(local_grad, 'x', scatter_dimension=0, tiled=True)
        grad_piece = lax.psum(grad_piece, ('z', 'y')) / n_dev
        return lax.all_gather(grad_piece, 'x', axis=0, tiled=True)

    def per_device(acts_in, grad_out, w_up1, w_down1, w_up2, w_down2):
        return local_backward(acts_in, grad_out, w_up1, w_down1, w_up2, w_down2, reduce_grad)

    return jax.shard_map(per_device, mesh=mesh, in_specs=(batch_spec, batch_spec, full_spec, full_spec, full_spec, full_spec), out_specs=(full_spec, full_spec, full_spec, full_spec, batch_spec), check_vma=False)
```

profile of v0, /device:TPU:1, one launch (start us, length us, event | category | flops | bytes accessed | tf_op | source)
XLA Modules:
  0.0 520.6 jit_solution(13428508584875442672)
XLA Ops:
  7.2 0.0 reduce-scatter.11.cloned.1.call-start
  7.2 1.5 copy-done
  8.8 41.4 %fusion.2 = (bf16[2048,2048]{1,0:T(8,128)(2,1)S(1)}, bf16[2048,2048]{1,0:T(8,128)(2,1)}) fusion(bf16[2048,512]{1,0:T(8,128)(2,1)} %param.6, bf16[512,2048]{1,0:T(8,128)(2,1)S(1)} %copy-done), kind=kOutput, calls=%fused_computation.16 | convolution fusion | flops 4575985664 | bytes 20971520 | tf_op jit(solution)/shard_map/dot_general | solution.py:18
  50.1 3.2 copy-done.16
  53.4 4.7 add_convert_fusion.2
  58.1 4.7 convolution_convert_fusion
  62.9 3.3 copy-done.14
  66.1 39.3 %fusion.78 = f32[2048,512]{1,0:T(8,128)} fusion(bf16[2048,512]{1,0:T(8,128)(2,1)S(1)} %copy-done.4, bf16[2048,2048]{1,0:T(8,128)(2,1)S(1)} %convolution_convert_fusion), kind=kOutput, calls=%fused_computation.92 | convolution fusion | flops 4571791360 | bytes 14680064 | tf_op jit(solution)/shard_map/dot_general | solution.py:22
  105.4 0.0 reduce-scatter.13.cloned.1.call-start
  105.5 13.5 %fusion.76 = bf16[2048,2048]{1,0:T(8,128)(2,1)S(1)} fusion(bf16[2048,2048]{1,0:T(8,128)(2,1)} %copy-done.14, bf16[2048,512]{1,0:T(8,128)(2,1)} %param.7, bf16[2048,512]{1,0:T(8,128)(2,1)} %param.11), kind=kOutput, calls=%fused_computation.90 | convolution fusion | flops 4349493248 | bytes 20971520 | tf_op jit(solution)/shard_map/dot_general | solution.py:22
  119.1 5.1 add_convert_fusion.1
  124.2 2.6 copy-done.18
  126.8 9.3 %fusion.77 = bf16[2048,2048]{1,0:T(8,128)(2,1)S(1)} fusion(bf16[2048,2048]{1,0:T(8,128)(2,1)S(1)} %copy-done.18, bf16[2048,512]{1,0:T(8,128)(2,1)S(1)} %add_convert_fusion.1, bf16[2048,512]{1,0:T(8,128)(2,1)S(1)} %copy-done.9), kind=kOutput, calls=%fused_computation.91 | convolution fusion | flops 4349493248 | bytes 20971520 | tf_op jit(solution)/shard_map/dot_general | solution.py:22
  136.1 3.3 copy-done.15
  139.4 6.1 %convolution_bitcast_fusion = f32[512,2048]{0,1:T(8,128)} fusion(bf16[2048,2048]{1,0:T(8,128)(2,1)S(1)} %fusion.77, bf16[2048,512]{1,0:T(8,128)(2,1)S(1)} %copy-done.11), kind=kOutput, calls=%fused_computation.98 | convolution fusion | flops 4294967296 | bytes 14680064 | tf_op jit(solution)/shard_map/dot_general | solution.py:22
  145.5 5.3 %copy.21 = f32[512,2048]{1,0:T(8,128)} copy(f32[512,2048]{0,1:T(8,128)} %convolution_bitcast_fusion) | data formatting | bytes 8388608
  150.8 0.0 reduce-scatter.13.cloned.1.call-update
  150.8 0.3 reduce-scatter.9.cloned.1.call-start
  151.1 10.5 %fusion.110 = f32[2048,512]{1,0:T(8,128)} fusion(bf16[2048,2048]{1,0:T(8,128)(2,1)} %copy-done.16, bf16[2048,512]{1,0:T(8,128)(2,1)} %copy-done.17), kind=kOutput, calls=%fused_computation.133 | convolution fusion | flops 4294967296 | bytes 14680064 | tf_op jit(solution)/shard_map/dot_general | solution.py:22
  161.7 0.0 reduce-scatter.15.cloned.1.call-start
  161.8 10.6 %fusion.111 = f32[512,2048]{1,0:T(8,128)} fusion(bf16[2048,512]{1,0:T(8,128)(2,1)} %copy-done.13, bf16[2048,2048]{1,0:T(8,128)(2,1)} %copy-done.12), kind=kOutput, calls=%fused_computation.134 | convolution fusion | flops 4294967296 | bytes 14680064
  172.4 0.0 all-reduce.3.cloned.1.call-start
  172.4 0.0 reduce-scatter.11.cloned.1.call-done
  172.5 16.8 %reduce-scatter.13.cloned.1.call-done = f32[64,2048]{1,0:T(8,128)} async-done(((f32[512,2048]{1,0:T(8,128)}), f32[64,2048]{1,0:T(8,128)}) %reduce-scatter.13.cloned.1.call-update) | async-done | bytes 524304 | tf_op jit(solution)/shard_map/reduce_scatter | solution.py:50
  189.2 39.8 %reduce-scatter.9.cloned.1.call-done = f32[256,512]{1,0:T(8,128)} async-done(((f32[2048,512]{1,0:T(8,128)}), f32[256,512]{1,0:T(8,128)}) %reduce-scatter.9.cloned.1.call-update) | async-done | bytes 524304 | tf_op jit(solution)/shard_map/reduce_scatter | solution.py:50
  229.0 39.6 %reduce-scatter.15.cloned.1.call-done = f32[64,2048]{1,0:T(8,128)} async-done(((f32[512,2048]{1,0:T(8,128)}), f32[64,2048]{1,0:T(8,128)}) %reduce-scatter.15.cloned.1.call-update) | async-done | bytes 524304 | tf_op jit(solution)/shard_map/reduce_scatter | solution.py:50
  268.7 0.0 all-reduce.3.cloned.1.call-update
  268.7 0.0 all-gather.5.cloned.1.call-start
  268.7 95.0 %all-reduce.3.cloned.1.call-done = (f32[64,2048]{1,0:T(8,128)}, f32[256,512]{1,0:T(8,128)}, f32[64,2048]{1,0:T(8,128)}, f32[256,512]{1,0:T(8,128)}) async-done(((f32[64,2048]{1,0:T(8,128)}, f32[256,512]{1,0:T(8,128)}, f32[64,2048]{1,0:T(8,128)}, f32[256,512]{1,0:T(8,128)}), (f32[64,2048]{1,0:T(8,128)}, f32[256,512]{1,0:T(8,128)}, f32[64,2048]{1,0:T(8,128)}, ...) | async-done | bytes 2097168 | tf_op jit(solution)/shard_map/psum | solution.py:51
  363.7 1.9 broadcast_multiply_fusion.3
  365.6 0.0 all-gather.7.cloned.1.call-start
  365.6 1.9 broadcast_multiply_fusion.1
  367.5 0.0 all-gather.7.cloned.1.call-update
  367.5 0.0 all-gather.9.cloned.1.call-start
  367.6 1.9 broadcast_multiply_fusion.2
  369.5 0.0 all-gather.9.cloned.1.call-update
  369.5 0.0 all-gather.11.cloned.1.call-start
  369.5 1.9 broadcast_multiply_fusion
  371.4 9.5 %add_convert_fusion = bf16[2048,512]{1,0:T(8,128)(2,1)} fusion(bf16[2048,512]{1,0:T(8,128)(2,1)} %copy-done.17, bf16[2048,2048]{1,0:T(8,128)(2,1)} %copy-done.15, bf16[512,2048]{1,0:T(8,128)(2,1)S(1)} %copy-done), kind=kOutput, calls=%fused_computation.95 | convolution fusion | flops 4298113024 | bytes 14680064 | tf_op jit(solution)/shard_map/dot_general | solution.py:22
  381.0 17.8 %all-gather.5.cloned.1.call-done = f32[512,2048]{1,0:T(8,128)} async-done(((f32[64,2048]{1,0:T(8,128)}), f32[512,2048]{1,0:T(8,128)}) %all-gather.5.cloned.1.call-update) | async-done | bytes 4194320 | tf_op jit(solution)/shard_map/all_gather | solution.py:52
  398.8 34.1 %all-gather.7.cloned.1.call-done = f32[2048,512]{1,0:T(8,128)} async-done(((f32[256,512]{1,0:T(8,128)}), f32[2048,512]{1,0:T(8,128)}) %all-gather.7.cloned.1.call-update) | async-done | bytes 4194320 | tf_op jit(solution)/shard_map/all_gather | solution.py:52
  432.8 34.1 %all-gather.9.cloned.1.call-done = f32[512,2048]{1,0:T(8,128)} async-done(((f32[64,2048]{1,0:T(8,128)}), f32[512,2048]{1,0:T(8,128)}) %all-gather.9.cloned.1.call-update) | async-done | bytes 4194320 | tf_op jit(solution)/shard_map/all_gather | solution.py:52
  466.9 34.1 %all-gather.11.cloned.1.call-done = f32[2048,512]{1,0:T(8,128)} async-done(((f32[256,512]{1,0:T(8,128)}), f32[2048,512]{1,0:T(8,128)}) %all-gather.11.cloned.1.call-update) | async-done | bytes 4194320 | tf_op jit(solution)/shard_map/all_gather | solution.py:52
  500.9 5.0 copy.33
  505.9 2.1 copy.34
  508.1 2.1 copy.35
  510.2 1.4 copy-done.3
  511.6 2.0 copy.36
  (37 shorter events, 0.2 us)
Async XLA Ops:
  7.2 1.6 copy-start
  7.2 165.3 %reduce-scatter.11.cloned.1.call-start = ((), (), s32[]{:S(2)}) async-start(), calls=%async_computation.8 | async-start | bytes 4718592 | tf_op jit(solution)/shard_map/reduce_scatter | solution.py:50
  8.8 44.6 %copy-start.8 = (bf16[2048,512]{1,0:T(8,128)(2,1)S(1)}, bf16[2048,512]{1,0:T(8,128)(2,1)}, u32[]{:S(2)}) copy-start(bf16[2048,512]{1,0:T(8,128)(2,1)} %param.9) | copy-start | bytes 6291460
  8.8 44.6 %copy-start.10 = (bf16[2048,512]{1,0:T(8,128)(2,1)S(1)}, bf16[2048,512]{1,0:T(8,128)(2,1)}, u32[]{:S(2)}) copy-start(bf16[2048,512]{1,0:T(8,128)(2,1)} %param.6) | copy-start | bytes 6291460
  50.1 3.3 copy-start.16
  53.4 4.7 copy-start.6
  58.1 4.8 copy-start.13
  58.1 8.0 %copy-start.4 = (bf16[2048,512]{1,0:T(8,128)(2,1)S(1)}, bf16[2048,512]{1,0:T(8,128)(2,1)}, u32[]{:S(2)}) copy-start(bf16[2048,512]{1,0:T(8,128)(2,1)} %param.7) | copy-start | bytes 6291460
  62.9 3.3 copy-start.14
  105.4 83.8 %reduce-scatter.13.cloned.1.call-start = ((), (), s32[]{:S(2)}) async-start(), calls=%async_computation.10 | async-start | bytes 4718592 | tf_op jit(solution)/shard_map/reduce_scatter | solution.py:50
  105.5 13.5 %copy-start.5 = (bf16[2048,512]{1,0:T(8,128)(2,1)S(1)}, bf16[2048,512]{1,0:T(8,128)(2,1)}, u32[]{:S(2)}) copy-start(bf16[2048,512]{1,0:T(8,128)(2,1)} %param.7) | copy-start | bytes 6291460
  105.5 13.5 %copy-start.7 = (bf16[512,2048]{1,0:T(8,128)(2,1)S(1)}, bf16[512,2048]{1,0:T(8,128)(2,1)}, u32[]{:S(2)}) copy-start(bf16[512,2048]{1,0:T(8,128)(2,1)} %param.10) | copy-start | bytes 6291460
  119.0 5.2 copy-start.12
  119.0 5.2 copy-start.9
  119.1 7.8 %copy-start.18 = (bf16[2048,2048]{1,0:T(8,128)(2,1)S(1)}, bf16[2048,2048]{1,0:T(8,128)(2,1)}, u32[]{:S(2)}) copy-start(bf16[2048,2048]{1,0:T(8,128)(2,1)} %get-tuple-element.15) | copy-start | bytes 25165828
  124.2 11.9 %copy-start.17 = (bf16[2048,512]{1,0:T(8,128)(2,1)}, bf16[2048,512]{1,0:T(8,128)(2,1)S(1)}, u32[]{:S(2)}) copy-start(bf16[2048,512]{1,0:T(8,128)(2,1)S(1)} %add_convert_fusion.1) | copy-start | bytes 6291460
  126.8 12.6 %copy-start.11 = (bf16[2048,512]{1,0:T(8,128)(2,1)S(1)}, bf16[2048,512]{1,0:T(8,128)(2,1)}, u32[]{:S(2)}) copy-start(bf16[2048,512]{1,0:T(8,128)(2,1)} %param.6) | copy-start | bytes 6291460
  136.1 3.3 copy-start.15
  150.8 78.2 %reduce-scatter.9.cloned.1.call-start = ((), (), s32[]{:S(2)}) async-start(), calls=%async_computation.5 | async-start | bytes 4718592 | tf_op jit(solution)/shard_map/reduce_scatter | solution.py:50
  161.7 106.9 %reduce-scatter.15.cloned.1.call-start = ((), (), s32[]{:S(2)}) async-start(), calls=%async_computation.11 | async-start | bytes 4718592 | tf_op jit(solution)/shard_map/reduce_scatter | solution.py:50
  172.4 191.3 %all-reduce.3.cloned.1.call-start = ((), (), s32[]{:S(2)}) async-start(), calls=%async_computation.12 | async-start | bytes 4194304 | tf_op jit(solution)/shard_map/psum | solution.py:51
  268.7 130.1 %all-gather.5.cloned.1.call-start = ((), (), s32[]{:S(2)}) async-start(), calls=%async_computation.4 | async-start | bytes 4718592 | tf_op jit(solution)/shard_map/all_gather | solution.py:52
  365.6 67.3 %all-gather.7.cloned.1.call-start = ((), (), s32[]{:S(2)}) async-start(), calls=%async_computation.6 | async-start | bytes 4718592 | tf_op jit(solution)/shard_map/all_gather | solution.py:52
  367.5 99.4 %all-gather.9.cloned.1.call-start = ((), (), s32[]{:S(2)}) async-start(), calls=%async_computation.7 | async-start | bytes 4718592 | tf_op jit(solution)/shard_map/all_gather | solution.py:52
  369.5 131.5 %all-gather.11.cloned.1.call-start = ((), (), s32[]{:S(2)}) async-start(), calls=%async_computation.9 | async-start | bytes 4718592 | tf_op jit(solution)/shard_map/all_gather | solution.py:52
  500.9 5.0 copy-start.1
  500.9 7.1 %copy-start.2 = (f32[512,2048]{1,0:T(8,128)S(1)}, f32[512,2048]{1,0:T(8,128)}, u32[]{:S(2)}) copy-start(f32[512,2048]{1,0:T(8,128)} %all-gather.9.cloned.1.call-done) | copy-start | bytes 12582916
  505.9 5.7 %copy-start.3 = (f32[2048,512]{1,0:T(8,128)S(1)}, f32[2048,512]{1,0:T(8,128)}, u32[]{:S(2)}) copy-start(f32[2048,512]{1,0:T(8,128)} %all-gather.11.cloned.1.call-done) | copy-start | bytes 12582916
Sparse Core Ops, SparseCore 0:
  105.5 38.2 reduce-scatter.10
  150.9 38.2 reduce-scatter.12
  192.2 36.7 reduce-scatter.8
  231.8 36.7 reduce-scatter.14
  272.2 91.4 all-reduce.2
  365.8 32.9 all-gather.4
  401.1 31.7 all-gather.6
  435.1 31.7 all-gather.8
  469.2 31.7 all-gather.10
where the time goes:
time: 528 us; the launch traced here: 521 us
  waiting for transfers between devices  311 us (59%)
  matrix products  155 us (29%)
  local copies, waits for them, and re-layouts  32 us (6%)
  between operations  14.5 us (3%)
  other arithmetic  7.5 us (1%)
    all_gather x4, waiting for transfers between devices, reduce_grad(): return lax.all_gather(grad_piece, 'x', axis=0, tiled=True)  120 us
    reduce_scatter x4, waiting for transfers between devices, reduce_grad(): lax.psum_scatter(local_grad, 'x', scatter_dimension=0, tiled=True)  96.2 us
    psum x1, waiting for transfers between devices, reduce_grad(): grad_piece = lax.psum(grad_piece, ('z', 'y')) / n_dev  95 us
    dot_general x7, matrix products, contract(): return lax.dot_general(lhs, rhs, dims, preferred_element_type=jnp.float32)  93.3 us
    dot_general x3, matrix products, matmul(): return jnp.dot(lhs, rhs, preferred_element_type=jnp.float32)  50.8 us
    unnamed x43, local copies, waits for them, and re-layouts  32 us
    unnamed x1, matrix products  10.6 us
  transfers between devices with their start and end apart: 9, of which 8 were waited for; matrix products, arithmetic and copies ran while one was open for 15% of the time, Pallas kernels for 0%

commit v1 on v0

--- a/solution.py
+++ b/solution.py
@@ -8,6 +8,10 @@
 INV_ROOT_TWO_PI = 1.0 / math.sqrt(2.0 * math.pi)
 ROW_CONTRACT = (((0,), (0,)), ((), ()))
 COL_CONTRACT = (((1,), (1,)), ((), ()))
+
+
+def gelu(pre_act):
+    return 0.5 * pre_act * (1.0 + lax.erf(pre_act * INV_ROOT_TWO))
 
 
 def gelu_slope(pre_act):
@@ -24,10 +28,10 @@
 
 def local_backward(acts_local, grad_top, w_up1, w_down1, w_up2, w_down2, reduce_fn):
     pre_one = matmul(acts_local, w_up1).astype(jnp.bfloat16)
-    hid_one = jax.nn.gelu(pre_one.astype(jnp.float32), approximate=False).astype(jnp.bfloat16)
+    hid_one = gelu(pre_one.astype(jnp.float32)).astype(jnp.bfloat16)
     mid_res = (matmul(hid_one, w_down1) + acts_local.astype(jnp.float32)).astype(jnp.bfloat16)
     pre_two = matmul(mid_res, w_up2).astype(jnp.bfloat16)
-    hid_two = jax.nn.gelu(pre_two.astype(jnp.float32), approximate=False).astype(jnp.bfloat16)
+    hid_two = gelu(pre_two.astype(jnp.float32)).astype(jnp.bfloat16)
     gw_down2 = reduce_fn(contract(hid_two, grad_top, ROW_CONTRACT))
     grad_hid2 = contract(grad_top, w_down2, COL_CONTRACT).astype(jnp.bfloat16)
     grad_pre2 = (grad_hid2.astype(jnp.float32) * gelu_slope(pre_two.astype(jnp.float32))).astype(jnp.bfloat16)
@@ -47,9 +51,7 @@
     full_spec = P(None, None)
 
     def reduce_grad(local_grad):
-        grad_piece = lax.psum_scatter(local_grad, 'x', scatter_dimension=0, tiled=True)
-        grad_piece = lax.psum(grad_piece, ('z', 'y')) / n_dev
-        return lax.all_gather(grad_piece, 'x', axis=0, tiled=True)
+        return lax.psum(local_grad, ('z', 'y', 'x')) / n_dev
 
     def per_device(acts_in, grad_out, w_up1, w_down1, w_up2, w_down2):
         return local_backward(acts_in, grad_out, w_up1, w_down1, w_up2, w_down2, reduce_grad)

time: 528 us -> 370 us (0.70); the launches traced: 521 us -> 370 us
  waiting for transfers between devices: 311 us -> 211 us
  matrix products: 155 us -> 117 us
  local copies, waits for them, and re-layouts: 32 us -> 12.3 us
  other arithmetic: 7.5 us -> 15.8 us
    all_gather x4 -> x0, waiting for transfers between devices: 120 us -> none  [reduce_grad(): return lax.all_gather(grad_piece, 'x', axis=0, tiled=True)]
    psum x1, waiting for transfers between devices: 95 us -> 211 us  [reduce_grad(): return lax.psum(local_grad, ('z', 'y', 'x')) / n_dev]
    reduce_scatter x4 -> x0, waiting for transfers between devices: 96.2 us -> none  [reduce_grad(): lax.psum_scatter(local_grad, 'x', scatter_dimension=0, tiled=True)]
    unnamed x43 -> x18, local copies, waits for them, and re-layouts: 32 us -> 12.3 us
    dot_general x3, matrix products: 50.8 us -> 32.8 us  [matmul(): return jnp.dot(lhs, rhs, preferred_element_type=jnp.float32)]
    unnamed x1 -> x0, matrix products: 10.6 us -> none
    dot_general x7 -> x8, matrix products: 93.3 us -> 84.5 us  [contract(): return lax.dot_general(lhs, rhs, dims, preferred_element_type=jnp.float32)]
    div x4 -> x2, other arithmetic: 7.5 us -> 15.8 us  [reduce_grad(): return lax.psum(local_grad, ('z', 'y', 'x')) / n_dev]
  transfers between devices with their start and end apart: 9 -> 1, of which waited for: 8 -> 1; matrix products, arithmetic and copies ran while one was open for 15% -> 3% of each run, Pallas kernels for 0% -> 0%
where the time goes in v1:
time: 370 us
  waiting for transfers between devices  211 us (57%)
  matrix products  117 us (32%)
  other arithmetic  15.8 us (4%)
  between operations  14.1 us (4%)
  local copies, waits for them, and re-layouts  12.3 us (3%)
    psum x1, waiting for transfers between devices, reduce_grad(): return lax.psum(local_grad, ('z', 'y', 'x')) / n_dev  211 us
    dot_general x8, matrix products, contract(): return lax.dot_general(lhs, rhs, dims, preferred_element_type=jnp.float32)  84.5 us
    dot_general x3, matrix products, matmul(): return jnp.dot(lhs, rhs, preferred_element_type=jnp.float32)  32.8 us
    div x2, other arithmetic, reduce_grad(): return lax.psum(local_grad, ('z', 'y', 'x')) / n_dev  15.8 us
    unnamed x18, local copies, waits for them, and re-layouts  12.3 us
  transfers between devices with their start and end apart: 1, of which 1 were waited for; matrix products, arithmetic and copies ran while one was open for 3% of the time, Pallas kernels for 0%

profile of v1, /device:TPU:1, one launch (start us, length us, event | category | flops | bytes accessed | tf_op | source)
XLA Modules:
  0.0 370.0 jit_solution(6535840354310590525)
XLA Ops:
  7.2 0.0 copy-start
  7.2 0.0 all-reduce.3.cloned.1.call-start
  7.2 1.5 copy-done
  8.8 0.0 copy-start.4
  8.8 0.0 copy-start.5
  8.8 11.5 %fusion.3 = (f32[2048,2048]{1,0:T(8,128)}, bf16[2048,2048]{1,0:T(8,128)(2,1)}) fusion(bf16[2048,512]{1,0:T(8,128)(2,1)} %param.6, bf16[512,2048]{1,0:T(8,128)(2,1)S(1)} %copy-done), kind=kOutput, calls=%fused_computation.13 | convolution fusion | flops 4311744512 | bytes 29360128 | tf_op jit(solution)/shard_map/dot_general | solution.py:22
  20.2 0.0 copy-done.4
  20.2 0.0 copy-done.5
  20.2 0.0 copy-start.3
  20.3 14.9 %add_convert_fusion.2 = bf16[2048,512]{1,0:T(8,128)(2,1)} fusion(bf16[2048,512]{1,0:T(8,128)(2,1)S(1)} %copy-done.5, bf16[2048,512]{1,0:T(8,128)(2,1)S(1)} %copy-done.4, f32[2048,2048]{1,0:T(8,128)} %get-tuple-element.14, bf16[2048,2048]{1,0:T(8,128)(2,1)} %get-tuple-element.15), kind=kOutput, calls=%fused_computation.34 | convolution fusion | flops 4314890240 | bytes 31457280 | tf_op jit(solution)/shard_map/dot_general | solution.py:22
  35.1 0.0 copy-done.3
  35.1 0.0 copy-start.2
  35.2 6.5 %convolution_convert_fusion = bf16[2048,2048]{1,0:T(8,128)(2,1)S(1)} fusion(bf16[2048,512]{1,0:T(8,128)(2,1)} %add_convert_fusion.2, bf16[512,2048]{1,0:T(8,128)(2,1)S(1)} %copy-done.3), kind=kOutput, calls=%fused_computation.30 | convolution fusion | flops 4299161600 | bytes 12582912 | tf_op jit(solution)/shard_map/dot_general | solution.py:22
  41.6 0.0 copy-done.2
  41.7 0.0 copy-start.1
  41.7 6.2 %fusion.18 = f32[2048,512]{1,0:T(8,128)} fusion(bf16[2048,512]{1,0:T(8,128)(2,1)S(1)} %copy-done.2, bf16[2048,2048]{1,0:T(8,128)(2,1)S(1)} %convolution_convert_fusion), kind=kOutput, calls=%fused_computation.28 | convolution fusion | flops 4320133120 | bytes 14680064 | tf_op jit(solution)/shard_map/dot_general | solution.py:26
  47.9 0.0 copy-done.1
  47.9 10.3 %fusion.15 = bf16[2048,2048]{1,0:T(8,128)(2,1)} fusion(bf16[2048,2048]{1,0:T(8,128)(2,1)S(1)} %convolution_convert_fusion, bf16[2048,512]{1,0:T(8,128)(2,1)S(1)} %copy-done.2, bf16[2048,512]{1,0:T(8,128)(2,1)S(1)} %copy-done.1), kind=kOutput, calls=%fused_computation.25 | convolution fusion | flops 4349493248 | bytes 20971520 | tf_op jit(solution)/shard_map/dot_general | solution.py:26
  58.2 0.0 copy-start.6
  58.2 8.5 %add_convert_fusion.1 = bf16[2048,512]{1,0:T(8,128)(2,1)S(1)} fusion(bf16[2048,512]{1,0:T(8,128)(2,1)S(1)} %copy-done.2, bf16[2048,2048]{1,0:T(8,128)(2,1)} %fusion.15, bf16[512,2048]{1,0:T(8,128)(2,1)S(1)} %copy-done.3), kind=kOutput, calls=%fused_computation.33 | convolution fusion | flops 4298113024 | bytes 14680064 | tf_op jit(solution)/shard_map/dot_general | solution.py:26
  66.6 0.0 copy-done.6
  66.6 0.0 copy-start.7
  66.6 12.2 %fusion.26 = f32[512,2048]{0,1:T(8,128)} fusion(bf16[2048,512]{1,0:T(8,128)(2,1)S(1)} %copy-done.6, bf16[2048,2048]{1,0:T(8,128)(2,1)} %fusion.15), kind=kOutput, calls=%fused_computation.42 | convolution fusion | flops 4294967296 | bytes 14680064 | tf_op jit(solution)/shard_map/dot_general | solution.py:26
  78.9 0.0 copy-done.7
  78.9 12.6 %fusion.22 = f32[2048,512]{1,0:T(8,128)} fusion(bf16[2048,512]{1,0:T(8,128)(2,1)S(1)} %add_convert_fusion.1, f32[2048,2048]{1,0:T(8,128)} %get-tuple-element.14, bf16[2048,2048]{1,0:T(8,128)(2,1)} %get-tuple-element.15), kind=kOutput, calls=%fused_computation.41 | convolution fusion | flops 4311744512 | bytes 31457280 | tf_op jit(solution)/shard_map/dot_general | solution.py:26
  91.5 15.4 %fusion.8 = bf16[2048,2048]{1,0:T(8,128)(2,1)} fusion(bf16[2048,2048]{1,0:T(8,128)(2,1)} %get-tuple-element.15, f32[2048,2048]{1,0:T(8,128)} %get-tuple-element.14, bf16[2048,512]{1,0:T(8,128)(2,1)} %copy-done.7, bf16[2048,512]{1,0:T(8,128)(2,1)S(1)} %copy-done.4), kind=kOutput, calls=%fused_computation.18 | convolution fusion | flops 4341104640 | bytes 37748736 | tf_op jit(solution)/shard_map/dot_general | solution.py:26
  106.9 9.7 %convolution_bitcast_fusion = f32[512,2048]{0,1:T(8,128)} fusion(bf16[2048,2048]{1,0:T(8,128)(2,1)} %fusion.8, bf16[2048,512]{1,0:T(8,128)(2,1)S(1)} %copy-done.5), kind=kOutput, calls=%fused_computation.35 | convolution fusion | flops 4294967296 | bytes 14680064 | tf_op jit(solution)/shard_map/dot_general | solution.py:26
  116.7 0.0 all-reduce.3.cloned.1.call-update
  116.7 9.5 %add_convert_fusion = bf16[2048,512]{1,0:T(8,128)(2,1)} fusion(bf16[2048,512]{1,0:T(8,128)(2,1)} %copy-done.7, bf16[2048,2048]{1,0:T(8,128)(2,1)} %fusion.8, bf16[512,2048]{1,0:T(8,128)(2,1)S(1)} %copy-done), kind=kOutput, calls=%fused_computation.32 | convolution fusion | flops 4298113024 | bytes 14680064 | tf_op jit(solution)/shard_map/dot_general | solution.py:26
  126.2 210.5 %all-reduce.3.cloned.1.call-done = (f32[512,2048]{0,1:T(8,128)}, f32[2048,512]{1,0:T(8,128)}, f32[512,2048]{0,1:T(8,128)}, f32[2048,512]{1,0:T(8,128)}) async-done(((f32[512,2048]{0,1:T(8,128)}, f32[2048,512]{1,0:T(8,128)}, f32[512,2048]{0,1:T(8,128)}, f32[2048,512]{1,0:T(8,128)}), (f32[512,2048]{0,1:T(8,128)}, f32[2048,512]{1,0:T(8,128)}, f32[512,2048]{0,1:T(8,128)}, ...) | async-done | bytes 16777232 | tf_op jit(solution)/shard_map/psum | solution.py:54
  336.7 7.9 %broadcast_multiply_fusion.2 = (f32[512,2048]{0,1:T(8,128)}, f32[512,2048]{0,1:T(8,128)}) fusion(f32[512,2048]{0,1:T(8,128)} %get-tuple-element.12, f32[512,2048]{0,1:T(8,128)} %get-tuple-element.10), kind=kLoop, calls=%fused_computation.38 | loop fusion | flops 2097152 | bytes 16777216 | tf_op jit(solution)/shard_map/div | solution.py:54
  344.6 5.3 %copy.13 = f32[512,2048]{1,0:T(8,128)} copy(f32[512,2048]{0,1:T(8,128)} %get-tuple-element.18) | data formatting | bytes 8388608
  350.0 5.3 %copy.12 = f32[512,2048]{1,0:T(8,128)} copy(f32[512,2048]{0,1:T(8,128)} %get-tuple-element.19) | data formatting | bytes 8388608
  355.3 7.9 %broadcast_multiply_fusion = (f32[2048,512]{1,0:T(8,128)}, f32[2048,512]{1,0:T(8,128)}) fusion(f32[2048,512]{1,0:T(8,128)} %get-tuple-element.13, f32[2048,512]{1,0:T(8,128)} %get-tuple-element.11), kind=kLoop, calls=%fused_computation.36 | loop fusion | flops 2097152 | bytes 16777216 | tf_op jit(solution)/shard_map/div | solution.py:54
Async XLA Ops:
  7.2 1.6 copy-start
  7.2 329.5 %all-reduce.3.cloned.1.call-start = ((), (), s32[]{:S(2)}) async-start(), calls=%async_computation | async-start | bytes 33554432 | tf_op jit(solution)/shard_map/psum | solution.py:54
  8.8 11.5 %copy-start.4 = (bf16[2048,512]{1,0:T(8,128)(2,1)S(1)}, bf16[2048,512]{1,0:T(8,128)(2,1)}, u32[]{:S(2)}) copy-start(bf16[2048,512]{1,0:T(8,128)(2,1)} %param.9) | copy-start | bytes 6291460
  8.8 11.5 %copy-start.5 = (bf16[2048,512]{1,0:T(8,128)(2,1)S(1)}, bf16[2048,512]{1,0:T(8,128)(2,1)}, u32[]{:S(2)}) copy-start(bf16[2048,512]{1,0:T(8,128)(2,1)} %param.6) | copy-start | bytes 6291460
  20.2 14.9 %copy-start.3 = (bf16[512,2048]{1,0:T(8,128)(2,1)S(1)}, bf16[512,2048]{1,0:T(8,128)(2,1)}, u32[]{:S(2)}) copy-start(bf16[512,2048]{1,0:T(8,128)(2,1)} %param.10) | copy-start | bytes 6291460
  35.1 6.5 %copy-start.2 = (bf16[2048,512]{1,0:T(8,128)(2,1)S(1)}, bf16[2048,512]{1,0:T(8,128)(2,1)}, u32[]{:S(2)}) copy-start(bf16[2048,512]{1,0:T(8,128)(2,1)} %param.7) | copy-start | bytes 6291460
  41.7 6.2 %copy-start.1 = (bf16[2048,512]{1,0:T(8,128)(2,1)S(1)}, bf16[2048,512]{1,0:T(8,128)(2,1)}, u32[]{:S(2)}) copy-start(bf16[2048,512]{1,0:T(8,128)(2,1)} %param.11) | copy-start | bytes 6291460
  58.2 8.5 %copy-start.6 = (bf16[2048,512]{1,0:T(8,128)(2,1)S(1)}, bf16[2048,512]{1,0:T(8,128)(2,1)}, u32[]{:S(2)}) copy-start(bf16[2048,512]{1,0:T(8,128)(2,1)} %add_convert_fusion.2) | copy-start | bytes 6291460
  66.6 12.3 %copy-start.7 = (bf16[2048,512]{1,0:T(8,128)(2,1)}, bf16[2048,512]{1,0:T(8,128)(2,1)S(1)}, u32[]{:S(2)}) copy-start(bf16[2048,512]{1,0:T(8,128)(2,1)S(1)} %add_convert_fusion.1) | copy-start | bytes 6291460
Sparse Core Ops, SparseCore 0:
  116.8 219.8 all-reduce.2

commit v2 on v1

v2 whole, which is shorter than its diff:
```python
import functools
import math
import jax
import jax.numpy as jnp
from jax import lax
from jax.experimental import pallas as pl
from jax.experimental.pallas import tpu as pltpu
from jax.sharding import PartitionSpec as P

INV_ROOT_TWO = 1.0 / math.sqrt(2.0)
INV_ROOT_TWO_PI = 1.0 / math.sqrt(2.0 * math.pi)
MESH = pl.DeviceIdType.MESH
BF16 = jnp.bfloat16
F32 = jnp.float32

TOK, DM, FF = 2048, 512, 2048
NB = 4
CB = FF // NB
NQ = 2 * NB
TT = 512
NT = TOK // TT
ND = 5
ROWS = (128, 32, 8)
GROUPS = ((0, 2), (2, 1), (3, 1))
OFFS = ((0, 128, 256), (384, 416, 448), (480, 488, 496))


def dot_nn(a, b):
    return lax.dot_general(a, b, (((1,), (0,)), ((), ())), preferred_element_type=F32)


def dot_nt(a, b):
    return lax.dot_general(a, b, (((1,), (1,)), ((), ())), preferred_element_type=F32)


def dot_tn(a, b):
    return lax.dot_general(a, b, (((0,), (0,)), ((), ())), preferred_element_type=F32)


def gelu_and_slope(pre):
    cdf = 0.5 * (1.0 + lax.erf(pre * INV_ROOT_TWO))
    return pre * cdf, cdf + pre * jnp.exp(-0.5 * pre * pre) * INV_ROOT_TWO_PI


def gelu(pre):
    return pre * (0.5 * (1.0 + lax.erf(pre * INV_ROOT_TWO)))


def kernel(x_hbm, g_hbm, w1_hbm, w2_hbm, w3_hbm, w4_hbm,
           o1, o2, o3, o4, odx,
           xv, gv, w1, w2, w3, w4, a1, h2, dh2, da, hc,
           gb, drb, rbuf,
           in_sem, rsem, ssem, dsem_s, dsem_r, osem, xsem):
    z, y, x = lax.axis_index('z'), lax.axis_index('y'), lax.axis_index('x')
    core = lax.rem(x, 2)
    cx = lax.div(x, 2)
    partner = (z, y, x + 1 - 2 * core)

    def hot(d):
        return lax.div((2 - d) * (1 - d), 2), d * (2 - d), lax.div(d * (d - 1), 2)

    def pos(d):
        ox, oy, oz = hot(d)
        return cx * ox + y * oy + z * oz

    def nbr(d, e):
        ox, oy, oz = hot(d)
        return (lax.rem(z + e * oz + 4, 4), lax.rem(y + e * oy + 4, 4),
                lax.rem(cx + e * ox + 4, 4) * 2 + core)

    loads = []
    n = 0

    def load(src, dst):
        nonlocal n
        cp = pltpu.make_async_copy(src, dst, in_sem.at[n])
        cp.start()
        n += 1
        return cp

    ld_x = load(x_hbm, xv)
    ld_w1 = [load(w1_hbm.at[:, pl.ds(c * CB, CB)], w1.at[c]) for c in range(NB)]
    ld_w2 = [load(w2_hbm.at[pl.ds(c * CB, CB), :], w2.at[c]) for c in range(NB)]
    ld_w3 = [load(w3_hbm.at[:, pl.ds(c * CB, CB)], w3.at[c]) for c in range(NB)]
    ld_g = load(g_hbm, gv)
    ld_w4 = [load(w4_hbm.at[pl.ds(c * CB, CB), :], w4.at[c]) for c in range(NB)]

    barrier = pltpu.get_barrier_semaphore()
    peers = [partner] + [nbr(d, e) for d in range(3) for e in (1, -1)]
    for peer in peers:
        pl.semaphore_signal(barrier, inc=1, device_id=peer, device_id_type=MESH)
    pl.semaphore_wait(barrier, len(peers))

    ld_x.wait()
    for cp in ld_w1 + ld_w2:
        cp.wait()

    def fwd1(t, carry):
        rows = pl.ds(pl.multiple_of(t * TT, TT), TT)
        xt = xv[rows, :]
        acc = xt.astype(F32)
        for c in range(NB):
            pre = dot_nn(xt, w1[c]).astype(BF16)
            a1[c, rows, :] = pre
            acc = acc + dot_nn(gelu(pre.astype(F32)).astype(BF16), w2[c])
        h2[rows, :] = acc.astype(BF16)
        return carry

    lax.fori_loop(0, NT, fwd1, 0)
    for cp in ld_w3 + [ld_g] + ld_w4:
        cp.wait()

    def group(q, gi):
        u0, s = GROUPS[gi]
        rot = lax.rem(q + gi, 3)
        e = 1 - 2 * lax.rem(q + gi, 2)
        dims = [lax.rem(rot + k, 3) for k in range(3)]
        ps = [pos(d) for d in dims]
        base = [0, ps[0] * ROWS[0], ps[0] * ROWS[0] + ps[1] * ROWS[1]]
        return u0, s, e, dims, ps, base

    def piece(q, half, u0, s, start, length):
        return gb.at[q, half, pl.ds(u0, s), pl.ds(pl.multiple_of(start, 8), length), :]

    def rb(slot, u0, s, off, length):
        return rbuf.at[slot, pl.ds(u0, s), pl.ds(off, length), :]

    class Phase:
        def __init__(self, q, gi, k):
            self.u0, self.s, self.e, dims, ps, base = group(q, gi)
            self.q, self.gi, self.k = q, gi, k
            self.d, self.p, self.base = dims[k], ps[k], base[k]
            self.L = ROWS[k]
            self.slot = lax.rem(q, 2)
            self.dslot = lax.rem(q, ND)

        def rows(self, j):
            return self.base + lax.rem(self.p + j + 4, 4) * self.L

        def mine(self, j):
            return piece(self.q, core, self.u0, self.s, self.rows(j), self.L)

        def part(self, j):
            return drb.at[self.dslot, pl.ds(self.u0, self.s), pl.ds(pl.multiple_of(self.rows(j), 8), self.L), :]

        def pval(self, j):
            return (self.dslot, pl.ds(self.u0, self.s), pl.ds(pl.multiple_of(self.rows(j), 8), self.L), slice(None))

        def val(self, j):
            return (self.q, core, pl.ds(self.u0, self.s), pl.ds(pl.multiple_of(self.rows(j), 8), self.L), slice(None))

        def buf(self, i):
            return rb(self.slot, self.u0, self.s, OFFS[self.k][i], self.L)

        def bufval(self, i):
            return rbuf[self.slot, pl.ds(self.u0, self.s), pl.ds(OFFS[self.k][i], self.L), :]

        def copy(self, src, dst, i, toward):
            idx = self.k * 6 + i
            return pltpu.make_async_remote_copy(
                src_ref=src, dst_ref=dst, send_sem=ssem.at[self.slot, self.gi, idx],
                recv_sem=rsem.at[self.slot, self.gi, idx],
                device_id=nbr(self.d, toward), device_id_type=MESH)

        def far(self):
            return self.copy(self.part(2), self.buf(0), 0, self.e)

        def near(self):
            return self.copy(self.part(-self.e), self.buf(1), 1, -self.e)

        def comb(self):
            return self.copy(self.part(self.e), self.buf(2), 2, self.e)

        def own_fwd(self):
            return self.copy(self.mine(0), self.mine(0), 3, self.e)

        def own_bwd(self):
            return self.copy(self.mine(0), self.mine(0), 4, -self.e)

        def relay(self):
            return self.copy(self.mine(-self.e), self.mine(-self.e), 5, self.e)

    def rs_a(q, k):
        for gi in range(3):
            ph = Phase(q, gi, k)
            ph.far().start()
            ph.near().start()

    def rs_b(q, k):
        for gi in range(3):
            ph = Phase(q, gi, k)
            ph.far().wait_recv()
            ix = ph.pval(ph.e)
            drb[ix] = drb[ix] + ph.bufval(0)
            ph.comb().start()

    def rs_c(q, k):
        for gi in range(3):
            ph = Phase(q, gi, k)
            ph.near().wait_recv()
            ph.comb().wait_recv()
            ix = ph.pval(0)
            tot = drb[ix] + (ph.bufval(1) + ph.bufval(2))
            if k == 2:
                gb[ph.val(0)] = tot * (1.0 / 128.0)
            else:
                drb[ix] = tot
            ph.far().wait_send()
            ph.near().wait_send()
            ph.comb().wait_send()

    def ag_a(q, k):
        for gi in range(3):
            ph = Phase(q, gi, k)
            ph.own_fwd().start()
            ph.own_bwd().start()

    def ag_b(q, k):
        for gi in range(3):
            ph = Phase(q, gi, k)
            ph.own_fwd().wait_recv()
            ph.relay().start()

    def ag_c(q, k):
        for gi in range(3):
            ph = Phase(q, gi, k)
            ph.own_bwd().wait_recv()
            ph.relay().wait_recv()
            ph.own_fwd().wait_send()
            ph.own_bwd().wait_send()
            ph.relay().wait_send()

    def d2d(q, back):
        slot = lax.rem(q, 2)
        if back:
            src = dst = gb.at[q, core]
        else:
            src, dst = gb.at[q, 1 - core], drb.at[lax.rem(q, ND)]
        return pltpu.make_async_remote_copy(
            src_ref=src, dst_ref=dst, send_sem=dsem_s.at[slot, int(back)], recv_sem=dsem_r.at[slot, int(back)],
            device_id=partner, device_id_type=MESH)

    def outs(q, act):
        slot = lax.rem(q, 2)

        def move(down, up, c):
            for half in range(2):
                for u in range(4):
                    src = gb.at[q, half, u]
                    if half == 0:
                        dst = down.at[pl.ds(pl.multiple_of(c * CB, CB), CB), pl.ds(u * 128, 128)]
                    else:
                        dst = up.at[:, pl.ds(pl.multiple_of(c * CB + u * 128, 128), 128)]
                    act(pltpu.make_async_copy(src, dst, osem.at[slot, half * 4 + u]))

        @pl.when(q < NB)
        def _():
            move(o4, o3, q)

        @pl.when(q >= NB)
        def _():
            move(o2, o1, q - NB)

    def stage(s, q):
        if s == 0:
            d2d(q, False).start()
        elif s == 1:
            d2d(q, False).wait_recv()
            slot = lax.rem(q, ND)
            drb[slot] = gb[q, core] + drb[slot]
            d2d(q, False).wait_send()
            rs_a(q, 0)
        elif s == 2:
            rs_b(q, 0)
        elif s == 3:
            rs_c(q, 0)
            rs_a(q, 1)
        elif s == 4:
            rs_b(q, 1)
        elif s == 5:
            rs_c(q, 1)
            rs_a(q, 2)
        elif s == 6:
            rs_b(q, 2)
        elif s == 7:
            rs_c(q, 2)
            ag_a(q, 2)
        elif s == 8:
            ag_b(q, 2)
        elif s == 9:
            ag_c(q, 2)
            ag_a(q, 1)
        elif s == 10:
            ag_b(q, 1)
        elif s == 11:
            ag_c(q, 1)
            ag_a(q, 0)
        elif s == 12:
            ag_b(q, 0)
        elif s == 13:
            ag_c(q, 0)
            d2d(q, True).start()
        elif s == 14:
            d2d(q, True).wait_recv()
            d2d(q, True).wait_send()
            outs(q, lambda cp: cp.start())
        elif s == 15:
            outs(q, lambda cp: cp.wait())

    def tick(i, odd):
        top = 15 if odd else 14
        for s in range(top, -1, -2):
            q = i - (s + 1) // 2

            @pl.when((q >= 0) & (q < NQ))
            def _():
                stage(s, q)

    def tile2(c):
        def body(t, carry):
            rows = pl.ds(pl.multiple_of(t * TT, TT), TT)
            pre = dot_nn(h2[rows, :], w3[c]).astype(BF16).astype(F32)
            act, slope = gelu_and_slope(pre)
            hc[rows, :] = act.astype(BF16)
            up = dot_nt(gv[rows, :], w4[c]).astype(BF16).astype(F32)
            da[c, rows, :] = (up * slope).astype(BF16)
            return carry
        lax.fori_loop(0, NT, body, 0)

    def tile1(c):
        def body(t, carry):
            rows = pl.ds(pl.multiple_of(t * TT, TT), TT)
            pre = a1[c, rows, :].astype(F32)
            act, slope = gelu_and_slope(pre)
            hc[rows, :] = act.astype(BF16)
            up = dot_nt(dh2[rows, :], w2[c]).astype(BF16).astype(F32)
            da[c, rows, :] = (up * slope).astype(BF16)
            return carry
        lax.fori_loop(0, NT, body, 0)

    def wgrad(q, c, down_rhs, up_lhs):
        down = dot_tn(hc[...], down_rhs[...])
        for u in range(4):
            gb[q, 0, u] = down[:, u * 128:(u + 1) * 128]
        up = dot_tn(up_lhs[...], da[c])
        for u in range(4):
            gb[q, 1, u] = up[:, u * 128:(u + 1) * 128]

    def back_tile(t, w, res, dst):
        rows = pl.ds(pl.multiple_of(t * TT, TT), TT)
        acc = res[rows, :].astype(F32)
        for c in range(NB):
            acc = acc + dot_nt(da[c, rows, :], w[c])
        dst[rows, :] = acc.astype(BF16)

    def step(i, carry):
        @pl.when(i < NB)
        def _():
            tile2(i)

        @pl.when(i == NB)
        def _():
            def body(t, c):
                back_tile(t, w3, gv, dh2)
                return c
            lax.fori_loop(0, NT, body, 0)

        @pl.when((i >= NB) & (i < NQ))
        def _():
            tile1(i - NB)

        @pl.when((i >= NQ) & (i < NQ + NT))
        def _():
            back_tile(i - NQ, w1, dh2, h2)

        tick(i, True)

        @pl.when(i < NB)
        def _():
            wgrad(i, i, gv, h2)

        @pl.when((i >= NB) & (i < NQ))
        def _():
            wgrad(i, i - NB, dh2, xv)

        @pl.when(i == NQ + NT)
        def _():
            pltpu.make_async_copy(h2, odx, xsem).start()

        tick(i, False)
        return carry

    lax.fori_loop(0, 2 * NQ, step, 0)
    pltpu.make_async_copy(h2, odx, xsem).wait()


def solution(mesh):
    batch_spec = P(('z', 'y', 'x'), None)
    full_spec = P(None, None)

    def per_device(acts_in, grad_out, w_up1, w_down1, w_up2, w_down2):
        any_spec = pl.BlockSpec(memory_space=pl.ANY)
        up = jax.ShapeDtypeStruct((DM, FF), F32)
        down = jax.ShapeDtypeStruct((FF, DM), F32)
        return pl.pallas_call(
            kernel,
            out_shape=(up, down, up, down, jax.ShapeDtypeStruct((TOK, DM), BF16)),
            in_specs=[any_spec] * 6,
            out_specs=(any_spec,) * 5,
            scratch_shapes=[
                pltpu.VMEM((TOK, DM), BF16),
                pltpu.VMEM((TOK, DM), BF16),
                pltpu.VMEM((NB, DM, CB), BF16),
                pltpu.VMEM((NB, CB, DM), BF16),
                pltpu.VMEM((NB, DM, CB), BF16),
                pltpu.VMEM((NB, CB, DM), BF16),
                pltpu.VMEM((NB, TOK, CB), BF16),
                pltpu.VMEM((TOK, DM), BF16),
                pltpu.VMEM((TOK, DM), BF16),
                pltpu.VMEM((NB, TOK, CB), BF16),
                pltpu.VMEM((TOK, CB), BF16),
                pltpu.VMEM((NQ, 2, 4, 512, 128), F32),
                pltpu.VMEM((ND, 4, 512, 128), F32),
                pltpu.VMEM((2, 4, 504, 128), F32),
                pltpu.SemaphoreType.DMA((18,)),
                pltpu.SemaphoreType.DMA((2, 3, 18)),
                pltpu.SemaphoreType.DMA((2, 3, 18)),
                pltpu.SemaphoreType.DMA((2, 2)),
                pltpu.SemaphoreType.DMA((2, 2)),
                pltpu.SemaphoreType.DMA((2, 8)),
                pltpu.SemaphoreType.DMA,
            ],
            compiler_params=pltpu.CompilerParams(
                collective_id=0, has_side_effects=True, vmem_limit_bytes=67043328),
            cost_estimate=pl.CostEstimate(flops=12 * 2 * TOK * DM * FF, bytes_accessed=32 * 2**20, transcendentals=0),
        )(acts_in, grad_out, w_up1, w_down1, w_up2, w_down2)

    return jax.shard_map(per_device, mesh=mesh, in_specs=(batch_spec, batch_spec, full_spec, full_spec, full_spec, full_spec), out_specs=(full_spec, full_spec, full_spec, full_spec, batch_spec), check_vma=False)
```

time: 370 us -> 180 us (0.49)
  waiting for transfers between devices: 211 us -> 0 us
  Pallas kernels: 0 us -> 163 us
  matrix products: 117 us -> 0 us
  other arithmetic: 15.8 us -> 0 us
  between operations: 14.1 us -> 0.65 us
  local copies, waits for them, and re-layouts: 12.3 us -> 16.7 us
    psum x1 -> x0, waiting for transfers between devices: 211 us -> none  [reduce_grad(): return lax.psum(local_grad, ('z', 'y', 'x')) / n_dev]
    pallas_call x0 -> x1, Pallas kernels: none -> 163 us  [per_device(): pl.pallas_call(kernel, out_shape=(up, down, up, down, jax.ShapeDtypeStruc...]
    dot_general x11 -> x0, matrix products: 117 us -> none  [the longest x8 84.5 us: contract(): return lax.dot_general(lhs, rhs, dims, preferred_element_type=jnp.float32)]
    div x2 -> x0, other arithmetic: 15.8 us -> none  [reduce_grad(): return lax.psum(local_grad, ('z', 'y', 'x')) / n_dev]
    unnamed x18 -> x13, local copies, waits for them, and re-layouts: 12.3 us -> 16.7 us
  transfers between devices with their start and end apart: 1 -> 0, of which waited for: 1 -> 0; matrix products, arithmetic and copies ran while one was open for 3% -> 0% of each run, Pallas kernels for 0% -> 0%
where the time goes in v2:
time: 180 us
  Pallas kernels  163 us (91%)
  local copies, waits for them, and re-layouts  16.7 us (9%)
    pallas_call x1, Pallas kernels, per_device(): pl.pallas_call(kernel, out_shape=(up, down, up, down, jax.ShapeDtypeStruc...  163 us
    unnamed x13, local copies, waits for them, and re-layouts  16.7 us

profile of v2, /device:TPU:1, one launch (start us, length us, event | category | flops | bytes accessed | tf_op | source)
XLA Modules:
  0.0 180.2 jit_solution(100974466646858354)
XLA Ops:
  0.6 162.9 %shard_map.101 = (f32[512,2048]{1,0:T(8,128)}, f32[2048,512]{1,0:T(8,128)}, f32[512,2048]{1,0:T(8,128)}, f32[2048,512]{1,0:T(8,128)}, bf16[2048,512]{1,0:T(8,128)(2,1)}) custom-call(bf16[2048,512]{1,0:T(8,128)(2,1)} %x_hbm.1, bf16[2048,512]{1,0:T(8,128)(2,1)} %g_hbm.1, bf16[512,2048]{1,0:T(8,128)(2,1)} %w1_hbm.1, bf16[2048,512]{1,0:T(8,128)(2,1)} %w2_hbm.1, ...), custom_call_target="tpu_custom_call" | custom-call | flops 51539607552 | bytes 33554432 | tf_op jit(solution)/shard_map/pallas_call | solution.py:405
  163.5 0.0 copy-start.2
  163.5 4.8 %copy.16 = f32[512,2048]{1,0:T(8,128)} copy(f32[512,2048]{1,0:T(8,128)} %get-tuple-element.10) | data formatting | bytes 8388608
  168.4 0.0 copy-done.2
  168.4 0.0 copy-start.1
  168.4 2.1 %copy.17 = f32[2048,512]{1,0:T(8,128)} copy(f32[2048,512]{1,0:T(8,128)S(1)} %copy-done.2) | data formatting | bytes 8388608
  170.5 1.6 copy-done.1
  172.1 0.0 copy-start
  172.1 2.1 %copy.18 = f32[512,2048]{1,0:T(8,128)} copy(f32[512,2048]{1,0:T(8,128)S(1)} %copy-done.1) | data formatting | bytes 8388608
  174.2 1.6 copy-done
  175.8 0.0 copy-start.3
  175.8 2.1 %copy.19 = f32[2048,512]{1,0:T(8,128)} copy(f32[2048,512]{1,0:T(8,128)S(1)} %copy-done) | data formatting | bytes 8388608
  177.9 1.0 copy-done.3
  178.9 1.3 copy.20
Async XLA Ops:
  163.5 4.9 %copy-start.2 = (f32[2048,512]{1,0:T(8,128)S(1)}, f32[2048,512]{1,0:T(8,128)}, u32[]{:S(2)}) copy-start(f32[2048,512]{1,0:T(8,128)} %get-tuple-element.11) | copy-start | bytes 12582916
  168.4 3.7 %copy-start.1 = (f32[512,2048]{1,0:T(8,128)S(1)}, f32[512,2048]{1,0:T(8,128)}, u32[]{:S(2)}) copy-start(f32[512,2048]{1,0:T(8,128)} %get-tuple-element.12) | copy-start | bytes 12582916
  172.1 3.7 %copy-start = (f32[2048,512]{1,0:T(8,128)S(1)}, f32[2048,512]{1,0:T(8,128)}, u32[]{:S(2)}) copy-start(f32[2048,512]{1,0:T(8,128)} %get-tuple-element.13) | copy-start | bytes 12582916
  175.8 3.1 %copy-start.3 = (bf16[2048,512]{1,0:T(8,128)(2,1)S(1)}, bf16[2048,512]{1,0:T(8,128)(2,1)}, u32[]{:S(2)}) copy-start(bf16[2048,512]{1,0:T(8,128)(2,1)} %get-tuple-element.14) | copy-start | bytes 6291460

commit v3 on v2

--- a/solution.py
+++ b/solution.py
@@ -19,7 +19,10 @@
 NQ = 2 * NB
 TT = 512
 NT = TOK // TT
-ND = 5
+ND = 6
+SL = 3
+PER, DIST = 3, 2
+DIRECT = (False, True, True)
 ROWS = (128, 32, 8)
 GROUPS = ((0, 2), (2, 1), (3, 1))
 OFFS = ((0, 128, 256), (384, 416, 448), (480, 488, 496))
@@ -47,10 +50,10 @@
 
 
 def kernel(x_hbm, g_hbm, w1_hbm, w2_hbm, w3_hbm, w4_hbm,
-           o1, o2, o3, o4, odx,
-           xv, gv, w1, w2, w3, w4, a1, h2, dh2, da, hc,
-           gb, drb, rbuf,
-           in_sem, rsem, ssem, dsem_s, dsem_r, osem, xsem):
+           gb, h2,
+           xv, gv, w1, w2, w3, w4, a1, dh2, da, hc,
+           drb, rbuf,
+           in_sem, rsem, ssem, dsem_s, dsem_r):
     z, y, x = lax.axis_index('z'), lax.axis_index('y'), lax.axis_index('x')
     core = lax.rem(x, 2)
     cx = lax.div(x, 2)
@@ -86,7 +89,7 @@
     ld_w4 = [load(w4_hbm.at[pl.ds(c * CB, CB), :], w4.at[c]) for c in range(NB)]
 
     barrier = pltpu.get_barrier_semaphore()
-    peers = [partner] + [nbr(d, e) for d in range(3) for e in (1, -1)]
+    peers = [partner] + [nbr(d, e) for d in range(3) for e in (1, -1, 2)]
     for peer in peers:
         pl.semaphore_signal(barrier, inc=1, device_id=peer, device_id_type=MESH)
     pl.semaphore_wait(barrier, len(peers))
@@ -131,7 +134,7 @@
             self.q, self.gi, self.k = q, gi, k
             self.d, self.p, self.base = dims[k], ps[k], base[k]
             self.L = ROWS[k]
-            self.slot = lax.rem(q, 2)
+            self.slot = lax.rem(q, SL)
             self.dslot = lax.rem(q, ND)
 
         def rows(self, j):
@@ -163,7 +166,7 @@
                 device_id=nbr(self.d, toward), device_id_type=MESH)
 
         def far(self):
-            return self.copy(self.part(2), self.buf(0), 0, self.e)
+            return self.copy(self.part(2), self.buf(0), 0, 2 if DIRECT[self.k] else self.e)
 
         def near(self):
             return self.copy(self.part(-self.e), self.buf(1), 1, -self.e)
@@ -178,6 +181,8 @@
             return self.copy(self.mine(0), self.mine(0), 4, -self.e)
 
         def relay(self):
+            if DIRECT[self.k]:
+                return self.copy(self.mine(0), self.mine(0), 5, 2)
             return self.copy(self.mine(-self.e), self.mine(-self.e), 5, self.e)
 
     def rs_a(q, k):
@@ -185,6 +190,8 @@
             ph = Phase(q, gi, k)
             ph.far().start()
             ph.near().start()
+            if DIRECT[k]:
+                ph.comb().start()
 
     def rs_b(q, k):
         for gi in range(3):
@@ -201,6 +208,9 @@
             ph.comb().wait_recv()
             ix = ph.pval(0)
             tot = drb[ix] + (ph.bufval(1) + ph.bufval(2))
+            if DIRECT[k]:
+                ph.far().wait_recv()
+                tot = tot + ph.bufval(0)
             if k == 2:
                 gb[ph.val(0)] = tot * (1.0 / 128.0)
             else:
@@ -214,6 +224,8 @@
             ph = Phase(q, gi, k)
             ph.own_fwd().start()
             ph.own_bwd().start()
+            if DIRECT[k]:
+                ph.relay().start()
 
     def ag_b(q, k):
         for gi in range(3):
@@ -224,6 +236,8 @@
     def ag_c(q, k):
         for gi in range(3):
             ph = Phase(q, gi, k)
+            if DIRECT[k]:
+                ph.own_fwd().wait_recv()
             ph.own_bwd().wait_recv()
             ph.relay().wait_recv()
             ph.own_fwd().wait_send()
@@ -231,7 +245,7 @@
             ph.relay().wait_send()
 
     def d2d(q, back):
-        slot = lax.rem(q, 2)
+        slot = lax.rem(q, SL)
         if back:
             src = dst = gb.at[q, core]
         else:
@@ -240,83 +254,50 @@
             src_ref=src, dst_ref=dst, send_sem=dsem_s.at[slot, int(back)], recv_sem=dsem_r.at[slot, int(back)],
             device_id=partner, device_id_type=MESH)
 
-    def outs(q, act):
-        slot = lax.rem(q, 2)
-
-        def move(down, up, c):
-            for half in range(2):
-                for u in range(4):
-                    src = gb.at[q, half, u]
-                    if half == 0:
-                        dst = down.at[pl.ds(pl.multiple_of(c * CB, CB), CB), pl.ds(u * 128, 128)]
-                    else:
-                        dst = up.at[:, pl.ds(pl.multiple_of(c * CB + u * 128, 128), 128)]
-                    act(pltpu.make_async_copy(src, dst, osem.at[slot, half * 4 + u]))
-
-        @pl.when(q < NB)
-        def _():
-            move(o4, o3, q)
-
-        @pl.when(q >= NB)
-        def _():
-            move(o2, o1, q - NB)
-
-    def stage(s, q):
-        if s == 0:
-            d2d(q, False).start()
-        elif s == 1:
-            d2d(q, False).wait_recv()
-            slot = lax.rem(q, ND)
-            drb[slot] = gb[q, core] + drb[slot]
-            d2d(q, False).wait_send()
-            rs_a(q, 0)
-        elif s == 2:
-            rs_b(q, 0)
-        elif s == 3:
-            rs_c(q, 0)
-            rs_a(q, 1)
-        elif s == 4:
-            rs_b(q, 1)
-        elif s == 5:
-            rs_c(q, 1)
-            rs_a(q, 2)
-        elif s == 6:
-            rs_b(q, 2)
-        elif s == 7:
-            rs_c(q, 2)
-            ag_a(q, 2)
-        elif s == 8:
-            ag_b(q, 2)
-        elif s == 9:
-            ag_c(q, 2)
-            ag_a(q, 1)
-        elif s == 10:
-            ag_b(q, 1)
-        elif s == 11:
-            ag_c(q, 1)
-            ag_a(q, 0)
-        elif s == 12:
-            ag_b(q, 0)
-        elif s == 13:
-            ag_c(q, 0)
-            d2d(q, True).start()
-        elif s == 14:
-            d2d(q, True).wait_recv()
-            d2d(q, True).wait_send()
-            outs(q, lambda cp: cp.start())
-        elif s == 15:
-            outs(q, lambda cp: cp.wait())
-
-    def tick(i, odd):
-        top = 15 if odd else 14
-        for s in range(top, -1, -2):
-            q = i - (s + 1) // 2
-
-            @pl.when((q >= 0) & (q < NQ))
-            def _():
-                stage(s, q)
-
-    def tile2(c):
+    def start_pair(q):
+        d2d(q, False).start()
+
+    def finish_pair(q):
+        d2d(q, False).wait_recv()
+        slot = lax.rem(q, ND)
+        drb[slot] = gb[q, core] + drb[slot]
+        d2d(q, False).wait_send()
+
+    def start_back(q):
+        d2d(q, True).start()
+
+    def finish_back(q):
+        d2d(q, True).wait_recv()
+        d2d(q, True).wait_send()
+
+    stages = [[start_pair]]
+    cur = [finish_pair]
+    for k in (0, 1, 2):
+        stages.append(cur + [functools.partial(rs_a, k=k)])
+        if not DIRECT[k]:
+            stages.append([functools.partial(rs_b, k=k)])
+        cur = [functools.partial(rs_c, k=k)]
+    for k in (2, 1, 0):
+        stages.append(cur + [functools.partial(ag_a, k=k)])
+        if not DIRECT[k]:
+            stages.append([functools.partial(ag_b, k=k)])
+        cur = [functools.partial(ag_c, k=k)]
+    stages.append(cur + [start_back])
+    stages.append([finish_back])
+    when = [PER - 1 + DIST * s for s in range(len(stages))]
+    n_iter = NQ + when[-1] // PER
+
+    def tick(i, j):
+        for s in reversed(range(len(stages))):
+            if when[s] % PER == j:
+                q = i - when[s] // PER
+
+                @pl.when((q >= 0) & (q < NQ))
+                def _():
+                    for f in stages[s]:
+                        f(q)
+
+    def tile2(c, lo, hi):
         def body(t, carry):
             rows = pl.ds(pl.multiple_of(t * TT, TT), TT)
             pre = dot_nn(h2[rows, :], w3[c]).astype(BF16).astype(F32)
@@ -325,9 +306,9 @@
             up = dot_nt(gv[rows, :], w4[c]).astype(BF16).astype(F32)
             da[c, rows, :] = (up * slope).astype(BF16)
             return carry
-        lax.fori_loop(0, NT, body, 0)
-
-    def tile1(c):
+        lax.fori_loop(lo, hi, body, 0)
+
+    def tile1(c, lo, hi):
         def body(t, carry):
             rows = pl.ds(pl.multiple_of(t * TT, TT), TT)
             pre = a1[c, rows, :].astype(F32)
@@ -336,7 +317,7 @@
             up = dot_nt(dh2[rows, :], w2[c]).astype(BF16).astype(F32)
             da[c, rows, :] = (up * slope).astype(BF16)
             return carry
-        lax.fori_loop(0, NT, body, 0)
+        lax.fori_loop(lo, hi, body, 0)
 
     def wgrad(q, c, down_rhs, up_lhs):
         down = dot_tn(hc[...], down_rhs[...])
@@ -353,11 +334,7 @@
             acc = acc + dot_nt(da[c, rows, :], w[c])
         dst[rows, :] = acc.astype(BF16)
 
-    def step(i, carry):
-        @pl.when(i < NB)
-        def _():
-            tile2(i)
-
+    def back_all(i):
         @pl.when(i == NB)
         def _():
             def body(t, c):
@@ -365,15 +342,31 @@
                 return c
             lax.fori_loop(0, NT, body, 0)
 
-        @pl.when((i >= NB) & (i < NQ))
-        def _():
-            tile1(i - NB)
+    def step(i, carry):
+        back_all(i)
 
         @pl.when((i >= NQ) & (i < NQ + NT))
         def _():
             back_tile(i - NQ, w1, dh2, h2)
 
-        tick(i, True)
+        def part(j, c):
+            lo, hi = j * (NT // (PER - 1)), (j + 1) * (NT // (PER - 1))
+
+            @pl.when(i < NB)
+            def _():
+                tile2(i, lo, hi)
+
+            @pl.when((i >= NB) & (i < NQ))
+            def _():
+                tile1(i - NB, lo, hi)
+
+            for jj in range(PER - 1):
+                @pl.when(j == jj)
+                def _():
+                    tick(i, jj)
+            return c
+
+        lax.fori_loop(0, PER - 1, part, 0)
 
         @pl.when(i < NB)
         def _():
@@ -383,15 +376,25 @@
         def _():
             wgrad(i, i - NB, dh2, xv)
 
-        @pl.when(i == NQ + NT)
-        def _():
-            pltpu.make_async_copy(h2, odx, xsem).start()
-
-        tick(i, False)
+        tick(i, PER - 1)
         return carry
 
-    lax.fori_loop(0, 2 * NQ, step, 0)
-    pltpu.make_async_copy(h2, odx, xsem).wait()
+    lax.fori_loop(0, n_iter, step, 0)
+
+
+def finish(gb, dx, o1, o2, o3, o4, odx, sem):
+    copies = [pltpu.make_async_copy(dx, odx, sem.at[NQ * 8])]
+    for q in range(NQ):
+        down, up, c = (o4, o3, q) if q < NB else (o2, o1, q - NB)
+        for u in range(4):
+            cols = pl.ds(u * 128, 128)
+            copies.append(pltpu.make_async_copy(gb.at[q, 0, u], down.at[pl.ds(c * CB, CB), cols], sem.at[q * 8 + u]))
+            cols = pl.ds(c * CB + u * 128, 128)
+            copies.append(pltpu.make_async_copy(gb.at[q, 1, u], up.at[:, cols], sem.at[q * 8 + 4 + u]))
+    for cp in copies:
+        cp.start()
+    for cp in copies:
+        cp.wait()
 
 
 def solution(mesh):
@@ -402,11 +405,12 @@
         any_spec = pl.BlockSpec(memory_space=pl.ANY)
         up = jax.ShapeDtypeStruct((DM, FF), F32)
         down = jax.ShapeDtypeStruct((FF, DM), F32)
-        return pl.pallas_call(
+        vm_spec = pl.BlockSpec(memory_space=pltpu.VMEM)
+        grads, dx = pl.pallas_call(
             kernel,
-            out_shape=(up, down, up, down, jax.ShapeDtypeStruct((TOK, DM), BF16)),
+            out_shape=(pltpu.VMEM((NQ, 2, 4, 512, 128), F32), pltpu.VMEM((TOK, DM), BF16)),
             in_specs=[any_spec] * 6,
-            out_specs=(any_spec,) * 5,
+            out_specs=(vm_spec, vm_spec),
             scratch_shapes=[
                 pltpu.VMEM((TOK, DM), BF16),
                 pltpu.VMEM((TOK, DM), BF16),
@@ -416,23 +420,27 @@
                 pltpu.VMEM((NB, CB, DM), BF16),
                 pltpu.VMEM((NB, TOK, CB), BF16),
                 pltpu.VMEM((TOK, DM), BF16),
-                pltpu.VMEM((TOK, DM), BF16),
                 pltpu.VMEM((NB, TOK, CB), BF16),
                 pltpu.VMEM((TOK, CB), BF16),
-                pltpu.VMEM((NQ, 2, 4, 512, 128), F32),
                 pltpu.VMEM((ND, 4, 512, 128), F32),
-                pltpu.VMEM((2, 4, 504, 128), F32),
+                pltpu.VMEM((SL, 4, 504, 128), F32),
                 pltpu.SemaphoreType.DMA((18,)),
-                pltpu.SemaphoreType.DMA((2, 3, 18)),
-                pltpu.SemaphoreType.DMA((2, 3, 18)),
-                pltpu.SemaphoreType.DMA((2, 2)),
-                pltpu.SemaphoreType.DMA((2, 2)),
-                pltpu.SemaphoreType.DMA((2, 8)),
-                pltpu.SemaphoreType.DMA,
+                pltpu.SemaphoreType.DMA((SL, 3, 18)),
+                pltpu.SemaphoreType.DMA((SL, 3, 18)),
+                pltpu.SemaphoreType.DMA((SL, 2)),
+                pltpu.SemaphoreType.DMA((SL, 2)),
             ],
             compiler_params=pltpu.CompilerParams(
-                collective_id=0, has_side_effects=True, vmem_limit_bytes=67043328),
+                collective_id=0, has_side_effects=True, vmem_limit_bytes=int(45.5 * 2**20)),
             cost_estimate=pl.CostEstimate(flops=12 * 2 * TOK * DM * FF, bytes_accessed=32 * 2**20, transcendentals=0),
         )(acts_in, grad_out, w_up1, w_down1, w_up2, w_down2)
+        return pl.pallas_call(
+            finish,
+            out_shape=(up, down, up, down, jax.ShapeDtypeStruct((TOK, DM), BF16)),
+            in_specs=[vm_spec, vm_spec],
+            out_specs=(any_spec,) * 5,
+            scratch_shapes=[pltpu.SemaphoreType.DMA((NQ * 8 + 1,))],
+            compiler_params=pltpu.CompilerParams(vmem_limit_bytes=2**20),
+        )(grads, dx)
 
     return jax.shard_map(per_device, mesh=mesh, in_specs=(batch_spec, batch_spec, full_spec, full_spec, full_spec, full_spec), out_specs=(full_spec, full_spec, full_spec, full_spec, batch_spec), check_vma=False)

time: 180 us -> 143 us (0.79)
  Pallas kernels: 163 us -> 142 us
  local copies, waits for them, and re-layouts: 16.7 us -> 0 us
    pallas_call x1 -> x2, Pallas kernels: 163 us -> 142 us  [the longest x1 135 us: per_device(): pl.pallas_call(kernel, out_shape=(pltpu.VMEM((NQ, 2, 4, 512, 128), F32),...]
    unnamed x13 -> x0, local copies, waits for them, and re-layouts: 16.7 us -> none
where the time goes in v3:
time: 143 us
  Pallas kernels  142 us (99%)
    pallas_call x1, Pallas kernels, per_device(): pl.pallas_call(kernel, out_shape=(pltpu.VMEM((NQ, 2, 4, 512, 128), F32),...  135 us
    pallas_call x1, Pallas kernels, per_device(): pl.pallas_call(finish, out_shape=(up, down, up, down, jax.ShapeDtypeStruc...  6.97 us

profile of v3, /device:TPU:1, one launch (start us, length us, event | category | flops | bytes accessed | tf_op | source)
XLA Modules:
  0.0 142.5 jit_solution(6463994646284063868)
XLA Ops:
  0.6 134.9 %shard_map.101 = (f32[8,2,4,512,128]{4,3,2,1,0:T(8,128)S(1)}, bf16[2048,512]{1,0:T(8,128)(2,1)S(1)}) custom-call(bf16[2048,512]{1,0:T(8,128)(2,1)} %x_hbm.1, bf16[2048,512]{1,0:T(8,128)(2,1)} %g_hbm.1, bf16[512,2048]{1,0:T(8,128)(2,1)} %w1_hbm.1, bf16[2048,512]{1,0:T(8,128)(2,1)} %w2_hbm.1, bf16[512,2048]{1,0:T(8,128)(2,1)} %w3_hbm.1, bf16[2048,512]{1,0:T(8,128)(2,1)} %w4_hbm.1), custom_call_target="tpu_custom_call" | custom-call | flops 51539607552 | bytes 33554432 | tf_op jit(solution)/shard_map/pallas_call | solution.py:409
  135.6 7.0 %shard_map.102 = (f32[512,2048]{1,0:T(8,128)}, f32[2048,512]{1,0:T(8,128)}, f32[512,2048]{1,0:T(8,128)}, f32[2048,512]{1,0:T(8,128)}, bf16[2048,512]{1,0:T(8,128)(2,1)}) custom-call(f32[8,2,4,512,128]{4,3,2,1,0:T(8,128)S(1)} %get-tuple-element.7.gb, bf16[2048,512]{1,0:T(8,128)(2,1)S(1)} %get-tuple-element.8.dx), custom_call_target="tpu_custom_call" | custom-call | tf_op jit(solution)/shard_map/pallas_call | solution.py:437

commit v4 on v3

v4 whole, which is shorter than its diff:
```python
import functools
import math
import jax
import jax.numpy as jnp
from jax import lax
from jax.experimental import pallas as pl
from jax.experimental.pallas import tpu as pltpu
from jax.sharding import PartitionSpec as P

INV_ROOT_TWO = 1.0 / math.sqrt(2.0)
INV_ROOT_TWO_PI = 1.0 / math.sqrt(2.0 * math.pi)
HALF_LOG2_E = 0.5 / math.log(2.0)
SLOT3 = (0, 1, 2)
TAIL = (-1, -1, 7, 6, 5, 4, 3, 2, 1, -1, -1, 7, 6, 5, 4, 0, 3, 7, 6, 5, 2, 4, 7, 6, 5, 3, 2, 1, 7, 6, 4, 5, 7, 3, 6, 2, 4, 3, 5, 7, 6, 4, 5, 7, 5, 6, 7, 6, 7)
LOGICAL = pl.DeviceIdType.LOGICAL
BF16 = jnp.bfloat16
F32 = jnp.float32

TOK, DM, FF = 2048, 512, 2048
NB = 4
CB = FF // NB
NQ = 2 * NB
TT = 512
NT = TOK // TT
ND = 5
SL = 3
PER, DIST = 4, 3
DIRECT = (False, True, True)
ROWS = (128, 32, 8)
OUTER = ((0, 1, 0, 1), (1, 1, 0, 3), (2, 1, 1, 1), (3, 1, 2, 3))
INNER = ((0, 2, 0, 1), (2, 1, 1, 1), (3, 1, 2, 1))
OFFS = ((0, 128, 256), (384, 416, 448), (480, 488, 496))


def dot_nn(a, b):
    return lax.dot_general(a, b, (((1,), (0,)), ((), ())), preferred_element_type=F32)


def dot_nt(a, b):
    return lax.dot_general(a, b, (((1,), (1,)), ((), ())), preferred_element_type=F32)


def dot_tn(a, b):
    return lax.dot_general(a, b, (((0,), (0,)), ((), ())), preferred_element_type=F32)


def gelu_and_slope(pre):
    cdf = 0.5 * (1.0 + lax.erf(pre * INV_ROOT_TWO))
    return pre * cdf, cdf + pre * jnp.exp2(pre * pre * -HALF_LOG2_E) * INV_ROOT_TWO_PI


def gelu(pre):
    return pre * (0.5 * (1.0 + lax.erf(pre * INV_ROOT_TWO)))


def kernel(x_hbm, g_hbm, w1_hbm, w2_hbm, w3_hbm, w4_hbm,
           gb, h2,
           xv, gv, w1, w2, w3, w4, a1, dh2, da, hc,
           drb, rbuf,
           in_sem, rsem, ssem, dsem_s, dsem_r):
    z, y, x = lax.axis_index('z'), lax.axis_index('y'), lax.axis_index('x')
    core = lax.rem(x, 2)
    cx = lax.div(x, 2)
    me = z * 32 + y * 8 + x
    partner = me + 1 - 2 * core
    at = [[lax.rem(p + j, 4) for p in (cx, y, z)] for j in range(4)]
    dev = [[me + (at[j][d] - at[0][d]) * stride for d, stride in enumerate((2, 8, 32))] for j in range(4)]

    loads = []
    n = 0

    def load(src, dst):
        nonlocal n
        cp = pltpu.make_async_copy(src, dst, in_sem.at[n])
        cp.start()
        n += 1
        return cp

    ld_x = load(x_hbm, xv)
    ld_w1 = [load(w1_hbm.at[:, pl.ds(c * CB, CB)], w1.at[c]) for c in range(NB)]
    ld_w2 = [load(w2_hbm.at[pl.ds(c * CB, CB), :], w2.at[c]) for c in range(NB)]
    barrier = pltpu.get_barrier_semaphore()
    peers = [partner] + [dev[j][d] for j in (1, 2, 3) for d in range(3)]
    for peer in peers:
        pl.semaphore_signal(barrier, inc=1, device_id=peer, device_id_type=LOGICAL)

    ld_x.wait()
    for cp in ld_w1 + ld_w2:
        cp.wait()
    ld_w3 = [load(w3_hbm.at[:, pl.ds(c * CB, CB)], w3.at[c]) for c in range(NB)]
    ld_g = load(g_hbm, gv)
    ld_w4 = [load(w4_hbm.at[pl.ds(c * CB, CB), :], w4.at[c]) for c in range(NB)]

    def fwd1(t, carry):
        rows = pl.ds(pl.multiple_of(t * TT, TT), TT)
        xt = xv[rows, :]
        acc = xt.astype(F32)
        for c in range(NB):
            pre = dot_nn(xt, w1[c]).astype(BF16)
            a1[c, rows, :] = pre
            acc = acc + dot_nn(gelu(pre.astype(F32)).astype(BF16), w2[c])
        h2[rows, :] = acc.astype(BF16)
        return carry

    lax.fori_loop(0, NT, fwd1, 0)
    for cp in ld_w3 + [ld_g] + ld_w4:
        cp.wait()
    pl.semaphore_wait(barrier, len(peers))

    class Chunk:
        def __init__(self, q, select, dslot):
            self.q, self.select, self.dslot = q, select, dslot
            self.slot = select(SLOT3, 0)

    def static_chunk(q):
        return Chunk(q, lambda v, c: v[(q + c) % 3], q % ND)

    def dynamic_chunks(i):
        r, r6 = lax.rem(i, 3), lax.rem(i, ND)
        is0, is1 = r == 0, r == 1
        memo = {}

        def select(v, c):
            key = (id(v), c % 3)
            if key not in memo:
                a, b, d = v[c % 3], v[(c + 1) % 3], v[(c + 2) % 3]
                memo[key] = (jnp.where(is0, a, jnp.where(is1, b, d)), v)
            return memo[key][0]

        for v in at + dev:
            for c in range(3):
                select(v, c)
        for c in range(3):
            select(SLOT3, c)

        def make(back):
            t = r6 + (-back) % ND
            return Chunk(i - back, lambda v, c: select(v, c - back), jnp.where(t >= ND, t - ND, t))
        return make

    class Phase:
        def __init__(self, ch, gi, k):
            self.u0, self.s, rot, self.e = (INNER if DIRECT[k] else OUTER)[gi]
            self.ch, self.gi, self.k, self.c = ch, gi, k, rot + k
            self.L = ROWS[k]
            self.base = 0
            for kk in range(k):
                self.base = self.base + ch.select(at[0], rot + kk) * ROWS[kk]

        def place(self, j):
            start = self.base + self.ch.select(at[j % 4], self.c) * self.L
            return pl.ds(pl.multiple_of(start, 8), self.L)

        def mine(self, j):
            return gb.at[self.ch.q, core, pl.ds(self.u0, self.s), self.place(j), :]

        def part(self, j):
            return drb.at[self.ch.dslot, pl.ds(self.u0, self.s), self.place(j), :]

        def pval(self, j):
            return (self.ch.dslot, pl.ds(self.u0, self.s), self.place(j), slice(None))

        def val(self, j):
            return (self.ch.q, core, pl.ds(self.u0, self.s), self.place(j), slice(None))

        def buf(self, i):
            return rbuf.at[self.ch.slot, pl.ds(self.u0, self.s), pl.ds(OFFS[self.k][i], self.L), :]

        def bufval(self, i):
            return rbuf[self.ch.slot, pl.ds(self.u0, self.s), pl.ds(OFFS[self.k][i], self.L), :]

        def copy(self, src, dst, i, toward):
            idx = self.k * 6 + i
            return pltpu.make_async_remote_copy(
                src_ref=src, dst_ref=dst, send_sem=ssem.at[self.ch.dslot, self.gi, idx],
                recv_sem=rsem.at[self.ch.dslot, self.gi, idx],
                device_id=self.ch.select(dev[toward % 4], self.c), device_id_type=LOGICAL)

        def far(self):
            return self.copy(self.part(2), self.buf(0), 0, 2 if DIRECT[self.k] else self.e)

        def near(self):
            return self.copy(self.part((4 - self.e)), self.buf(1), 1, (4 - self.e))

        def comb(self):
            return self.copy(self.part(self.e), self.buf(2), 2, self.e)

        def own_fwd(self):
            return self.copy(self.mine(0), self.mine(0), 3, self.e)

        def own_bwd(self):
            return self.copy(self.mine(0), self.mine(0), 4, (4 - self.e))

        def relay(self):
            if DIRECT[self.k]:
                return self.copy(self.mine(0), self.mine(0), 5, 2)
            return self.copy(self.mine((4 - self.e)), self.mine((4 - self.e)), 5, self.e)

    def rs_a(ch, k):
        for gi in range(3 if DIRECT[k] else 4):
            ph = Phase(ch, gi, k)
            ph.far().start()
            ph.near().start()
            if DIRECT[k]:
                ph.comb().start()

    def rs_b(ch, k):
        for gi in range(3 if DIRECT[k] else 4):
            ph = Phase(ch, gi, k)
            ph.far().wait_recv()
            ix = ph.pval(ph.e)
            drb[ix] = drb[ix] + ph.bufval(0)
            ph.comb().start()

    def rs_c(ch, k):
        for gi in range(3 if DIRECT[k] else 4):
            ph = Phase(ch, gi, k)
            ph.near().wait_recv()
            ph.comb().wait_recv()
            ix = ph.pval(0)
            tot = drb[ix] + (ph.bufval(1) + ph.bufval(2))
            if DIRECT[k]:
                ph.far().wait_recv()
                tot = tot + ph.bufval(0)
            if k == 2:
                gb[ph.val(0)] = tot * (1.0 / 128.0)
            else:
                drb[ix] = tot
            ph.far().wait_send()
            ph.near().wait_send()
            ph.comb().wait_send()

    def ag_a(ch, k):
        for gi in range(3 if DIRECT[k] else 4):
            ph = Phase(ch, gi, k)
            ph.own_fwd().start()
            ph.own_bwd().start()
            if DIRECT[k]:
                ph.relay().start()

    def ag_b(ch, k):
        for gi in range(3 if DIRECT[k] else 4):
            ph = Phase(ch, gi, k)
            ph.own_fwd().wait_recv()
            ph.relay().start()

    def ag_c(ch, k):
        for gi in range(3 if DIRECT[k] else 4):
            ph = Phase(ch, gi, k)
            if DIRECT[k]:
                ph.own_fwd().wait_recv()
            ph.own_bwd().wait_recv()
            ph.relay().wait_recv()
            ph.own_fwd().wait_send()
            ph.own_bwd().wait_send()
            ph.relay().wait_send()

    def d2d(ch, back):
        if back:
            src = dst = gb.at[ch.q, core]
        else:
            src, dst = gb.at[ch.q, 1 - core], drb.at[ch.dslot]
        return pltpu.make_async_remote_copy(
            src_ref=src, dst_ref=dst, send_sem=dsem_s.at[ch.dslot, int(back)], recv_sem=dsem_r.at[ch.dslot, int(back)],
            device_id=partner, device_id_type=LOGICAL)

    def start_pair(ch):
        d2d(ch, False).start()

    def finish_pair(ch):
        d2d(ch, False).wait_recv()
        drb[ch.dslot] = gb[ch.q, core] + drb[ch.dslot]
        d2d(ch, False).wait_send()

    def start_back(ch):
        d2d(ch, True).start()

    def finish_back(ch):
        d2d(ch, True).wait_recv()
        d2d(ch, True).wait_send()

    stages = [[start_pair]]
    cur = [finish_pair]
    for k in (0, 1, 2):
        stages.append(cur + [functools.partial(rs_a, k=k)])
        if not DIRECT[k]:
            stages.append([functools.partial(rs_b, k=k)])
        cur = [functools.partial(rs_c, k=k)]
    for k in (2, 1, 0):
        stages.append(cur + [functools.partial(ag_a, k=k)])
        if not DIRECT[k]:
            stages.append([functools.partial(ag_b, k=k)])
        cur = [functools.partial(ag_c, k=k)]
    stages.append(cur + [start_back])
    stages.append([finish_back])
    when = [PER - 1 + DIST * s for s in range(len(stages))]

    def tick(make, j, i):
        for s in reversed(range(len(stages))):
            if when[s] % PER == j:
                back = when[s] // PER

                @pl.when((i >= back) if back else (i >= 0))
                def _():
                    ch = make(back)
                    for f in stages[s]:
                        f(ch)

    def tile2(c, t):
        rows = pl.ds(pl.multiple_of(t * TT, TT), TT)
        pre = dot_nn(h2[rows, :], w3[c]).astype(BF16).astype(F32)
        act, slope = gelu_and_slope(pre)
        hc[lax.rem(c, 2), rows, :] = act.astype(BF16)
        up = dot_nt(gv[rows, :], w4[c]).astype(BF16).astype(F32)
        da[c, rows, :] = (up * slope).astype(BF16)

    def tile1(c, t):
        rows = pl.ds(pl.multiple_of(t * TT, TT), TT)
        pre = a1[c, rows, :].astype(F32)
        act, slope = gelu_and_slope(pre)
        hc[lax.rem(c, 2), rows, :] = act.astype(BF16)
        up = dot_nt(dh2[rows, :], w2[c]).astype(BF16).astype(F32)
        da[c, rows, :] = (up * slope).astype(BF16)

    def wgrad(q, c, half, n, down_rhs, up_lhs):
        cols = pl.ds(pl.multiple_of(n * 256, 256), 256)
        if half == 0:
            prod = dot_tn(hc[lax.rem(c, 2)], down_rhs[:, cols])
        else:
            prod = dot_tn(up_lhs[...], da[c, :, cols])
        for u in range(2):
            gb[q, half, n * 2 + u] = prod[:, u * 128:(u + 1) * 128]

    def back_tile(t, w, res, dst):
        rows = pl.ds(t * TT if isinstance(t, int) else pl.multiple_of(t * TT, TT), TT)
        acc = res[rows, :].astype(F32)
        for c in range(NB):
            acc = acc + dot_nt(da[c, rows, :], w[c])
        dst[rows, :] = acc.astype(BF16)

    def step(i, carry):
        make = dynamic_chunks(i)

        @pl.when(i == NB)
        def _():
            def body(t, c):
                back_tile(t, w3, gv, dh2)
                tile1(0, t)
                return c
            lax.fori_loop(0, NT, body, 0)

        for half in range(2):
            def part(n, c):
                t = half * 2 + n

                @pl.when(i < NB - 1)
                def _():
                    wgrad(i, i, half, n, gv, h2)
                    tile2(i + 1, t)

                @pl.when(i == NB - 1)
                def _():
                    wgrad(i, i, half, n, gv, h2)

                @pl.when((i >= NB) & (i < NQ - 1))
                def _():
                    wgrad(i, i - NB, half, n, dh2, xv)
                    tile1(i - NB + 1, t)

                @pl.when(i == NQ - 1)
                def _():
                    wgrad(i, i - NB, half, n, dh2, xv)

                for jj in range(2):
                    @pl.when(n == jj)
                    def _():
                        tick(make, half * 2 + jj, i)
                return c

            lax.fori_loop(0, 2, part, 0)
        return carry

    def first(t, carry):
        tile2(0, t)
        return carry

    lax.fori_loop(0, NT, first, 0)
    lax.fori_loop(0, NQ, step, 0)

    done = [sum(w + PER * q < PER * NQ for w in when) for q in range(NQ)]
    tiles = 0
    for q in TAIL:
        if q < 0:
            back_tile(tiles, w1, dh2, h2)
            tiles += 1
        else:
            for f in stages[done[q]]:
                f(static_chunk(q))
            done[q] += 1
    assert tiles == NT and done == [len(stages)] * NQ


def finish(gb, dx, o1, o2, o3, o4, odx, sem):
    copies = [pltpu.make_async_copy(dx, odx, sem.at[NQ * 8])]
    for q in range(NQ):
        down, up, c = (o4, o3, q) if q < NB else (o2, o1, q - NB)
        for u in range(4):
            cols = pl.ds(u * 128, 128)
            copies.append(pltpu.make_async_copy(gb.at[q, 0, u], down.at[pl.ds(c * CB, CB), cols], sem.at[q * 8 + u]))
            cols = pl.ds(c * CB + u * 128, 128)
            copies.append(pltpu.make_async_copy(gb.at[q, 1, u], up.at[:, cols], sem.at[q * 8 + 4 + u]))
    for cp in copies:
        cp.start()
    for cp in copies:
        cp.wait()


def solution(mesh):
    batch_spec = P(('z', 'y', 'x'), None)
    full_spec = P(None, None)

    def per_device(acts_in, grad_out, w_up1, w_down1, w_up2, w_down2):
        any_spec = pl.BlockSpec(memory_space=pl.ANY)
        up = jax.ShapeDtypeStruct((DM, FF), F32)
        down = jax.ShapeDtypeStruct((FF, DM), F32)
        vm_spec = pl.BlockSpec(memory_space=pltpu.VMEM)
        grads, dx = pl.pallas_call(
            kernel,
            out_shape=(pltpu.VMEM((NQ, 2, 4, 512, 128), F32), pltpu.VMEM((TOK, DM), BF16)),
            in_specs=[any_spec] * 6,
            out_specs=(vm_spec, vm_spec),
            scratch_shapes=[
                pltpu.VMEM((TOK, DM), BF16),
                pltpu.VMEM((TOK, DM), BF16),
                pltpu.VMEM((NB, DM, CB), BF16),
                pltpu.VMEM((NB, CB, DM), BF16),
                pltpu.VMEM((NB, DM, CB), BF16),
                pltpu.VMEM((NB, CB, DM), BF16),
                pltpu.VMEM((NB, TOK, CB), BF16),
                pltpu.VMEM((TOK, DM), BF16),
                pltpu.VMEM((NB, TOK, CB), BF16),
                pltpu.VMEM((2, TOK, CB), BF16),
                pltpu.VMEM((ND, 4, 512, 128), F32),
                pltpu.VMEM((SL, 4, 504, 128), F32),
                pltpu.SemaphoreType.DMA((18,)),
                pltpu.SemaphoreType.DMA((ND, 4, 18)),
                pltpu.SemaphoreType.DMA((ND, 4, 18)),
                pltpu.SemaphoreType.DMA((ND, 2)),
                pltpu.SemaphoreType.DMA((ND, 2)),
            ],
            compiler_params=pltpu.CompilerParams(
                collective_id=0, has_side_effects=True, vmem_limit_bytes=int(45.9 * 2**20)),
            cost_estimate=pl.CostEstimate(flops=12 * 2 * TOK * DM * FF, bytes_accessed=32 * 2**20, transcendentals=0),
        )(acts_in, grad_out, w_up1, w_down1, w_up2, w_down2)
        return pl.pallas_call(
            finish,
            out_shape=(up, down, up, down, jax.ShapeDtypeStruct((TOK, DM), BF16)),
            in_specs=[vm_spec, vm_spec],
            out_specs=(any_spec,) * 5,
            scratch_shapes=[pltpu.SemaphoreType.DMA((NQ * 8 + 1,))],
            compiler_params=pltpu.CompilerParams(vmem_limit_bytes=2**20),
        )(grads, dx)

    return jax.shard_map(per_device, mesh=mesh, in_specs=(batch_spec, batch_spec, full_spec, full_spec, full_spec, full_spec), out_specs=(full_spec, full_spec, full_spec, full_spec, batch_spec), check_vma=False)
```

time: 143 us -> 139 us (0.972)
  Pallas kernels: 142 us -> 139 us
    pallas_call x1, Pallas kernels: 135 us -> 132 us  [per_device(): pl.pallas_call(kernel, out_shape=(pltpu.VMEM((NQ, 2, 4, 512, 128), F32),...]
where the time goes in v4:
time: 139 us
  Pallas kernels  139 us (100%)
    pallas_call x1, Pallas kernels, per_device(): pl.pallas_call(kernel, out_shape=(pltpu.VMEM((NQ, 2, 4, 512, 128), F32),...  132 us
    pallas_call x1, Pallas kernels, per_device(): pl.pallas_call(finish, out_shape=(up, down, up, down, jax.ShapeDtypeStruc...  6.97 us

profile of v4, /device:TPU:1, one launch (start us, length us, event | category | flops | bytes accessed | tf_op | source)
XLA Modules:
  0.0 139.4 jit_solution(16918297572702746680)
XLA Ops:
  0.6 131.6 %shard_map.101 = (f32[8,2,4,512,128]{4,3,2,1,0:T(8,128)S(1)}, bf16[2048,512]{1,0:T(8,128)(2,1)S(1)}) custom-call(bf16[2048,512]{1,0:T(8,128)(2,1)} %x_hbm.1, bf16[2048,512]{1,0:T(8,128)(2,1)} %g_hbm.1, bf16[512,2048]{1,0:T(8,128)(2,1)} %w1_hbm.1, bf16[2048,512]{1,0:T(8,128)(2,1)} %w2_hbm.1, bf16[512,2048]{1,0:T(8,128)(2,1)} %w3_hbm.1, bf16[2048,512]{1,0:T(8,128)(2,1)} %w4_hbm.1), custom_call_target="tpu_custom_call" | custom-call | flops 51539607552 | bytes 33554432 | tf_op jit(solution)/shard_map/pallas_call | solution.py:427
  132.2 7.0 %shard_map.102 = (f32[512,2048]{1,0:T(8,128)}, f32[2048,512]{1,0:T(8,128)}, f32[512,2048]{1,0:T(8,128)}, f32[2048,512]{1,0:T(8,128)}, bf16[2048,512]{1,0:T(8,128)(2,1)}) custom-call(f32[8,2,4,512,128]{4,3,2,1,0:T(8,128)S(1)} %get-tuple-element.7.gb, bf16[2048,512]{1,0:T(8,128)(2,1)S(1)} %get-tuple-element.8.dx), custom_call_target="tpu_custom_call" | custom-call | tf_op jit(solution)/shard_map/pallas_call | solution.py:455

commit v5 on v4

--- a/solution.py
+++ b/solution.py
@@ -170,11 +170,19 @@
             return rbuf[self.ch.slot, pl.ds(self.u0, self.s), pl.ds(OFFS[self.k][i], self.L), :]
 
         def copy(self, src, dst, i, toward):
-            idx = self.k * 6 + i
+            back = int(i >= 3)
+            if DIRECT[self.k]:
+                pair = ((self.k - 1) * 3 + self.gi) * 2 + back
+                si, ri = 8 + pair, 16 + pair
+            else:
+                si, ri = self.gi * 2 + back, self.gi * 4 + (0, 1, 1, 2, 3, 3)[i]
             return pltpu.make_async_remote_copy(
-                src_ref=src, dst_ref=dst, send_sem=ssem.at[self.ch.dslot, self.gi, idx],
-                recv_sem=rsem.at[self.ch.dslot, self.gi, idx],
+                src_ref=src, dst_ref=dst, send_sem=ssem.at[self.ch.dslot, si], recv_sem=rsem.at[self.ch.dslot, ri],
                 device_id=self.ch.select(dev[toward % 4], self.c), device_id_type=LOGICAL)
+
+        def whole(self, i, pieces):
+            ref = rbuf.at[self.ch.slot, pl.ds(self.u0, self.s), pl.ds(OFFS[self.k][0], pieces * self.L), :]
+            return self.copy(ref, ref, i, 1)
 
         def far(self):
             return self.copy(self.part(2), self.buf(0), 0, 2 if DIRECT[self.k] else self.e)
@@ -215,20 +223,19 @@
     def rs_c(ch, k):
         for gi in range(3 if DIRECT[k] else 4):
             ph = Phase(ch, gi, k)
-            ph.near().wait_recv()
-            ph.comb().wait_recv()
+            if DIRECT[k]:
+                ph.whole(0, 3).wait_recv()
+            else:
+                ph.whole(1, 2).wait_recv()
             ix = ph.pval(0)
             tot = drb[ix] + (ph.bufval(1) + ph.bufval(2))
             if DIRECT[k]:
-                ph.far().wait_recv()
                 tot = tot + ph.bufval(0)
             if k == 2:
                 gb[ph.val(0)] = tot * (1.0 / 128.0)
             else:
                 drb[ix] = tot
-            ph.far().wait_send()
-            ph.near().wait_send()
-            ph.comb().wait_send()
+            ph.whole(0, 3).wait_send()
 
     def ag_a(ch, k):
         for gi in range(3 if DIRECT[k] else 4):
@@ -248,12 +255,10 @@
         for gi in range(3 if DIRECT[k] else 4):
             ph = Phase(ch, gi, k)
             if DIRECT[k]:
-                ph.own_fwd().wait_recv()
-            ph.own_bwd().wait_recv()
-            ph.relay().wait_recv()
-            ph.own_fwd().wait_send()
-            ph.own_bwd().wait_send()
-            ph.relay().wait_send()
+                ph.whole(3, 3).wait_recv()
+            else:
+                ph.whole(4, 2).wait_recv()
+            ph.whole(3, 3).wait_send()
 
     def d2d(ch, back):
         if back:
@@ -401,18 +406,16 @@
 
 
 def finish(gb, dx, o1, o2, o3, o4, odx, sem):
-    copies = [pltpu.make_async_copy(dx, odx, sem.at[NQ * 8])]
+    pltpu.make_async_copy(dx, odx, sem.at[4]).start()
     for q in range(NQ):
-        down, up, c = (o4, o3, q) if q < NB else (o2, o1, q - NB)
+        (down, ds), (up, us), c = ((o4, 3), (o3, 2), q) if q < NB else ((o2, 1), (o1, 0), q - NB)
         for u in range(4):
             cols = pl.ds(u * 128, 128)
-            copies.append(pltpu.make_async_copy(gb.at[q, 0, u], down.at[pl.ds(c * CB, CB), cols], sem.at[q * 8 + u]))
+            pltpu.make_async_copy(gb.at[q, 0, u], down.at[pl.ds(c * CB, CB), cols], sem.at[ds]).start()
             cols = pl.ds(c * CB + u * 128, 128)
-            copies.append(pltpu.make_async_copy(gb.at[q, 1, u], up.at[:, cols], sem.at[q * 8 + 4 + u]))
-    for cp in copies:
-        cp.start()
-    for cp in copies:
-        cp.wait()
+            pltpu.make_async_copy(gb.at[q, 1, u], up.at[:, cols], sem.at[us]).start()
+    for n, out in enumerate((o1, o2, o3, o4, odx)):
+        pltpu.make_async_copy(out, out, sem.at[n]).wait()
 
 
 def solution(mesh):
@@ -443,8 +446,8 @@
                 pltpu.VMEM((ND, 4, 512, 128), F32),
                 pltpu.VMEM((SL, 4, 504, 128), F32),
                 pltpu.SemaphoreType.DMA((18,)),
-                pltpu.SemaphoreType.DMA((ND, 4, 18)),
-                pltpu.SemaphoreType.DMA((ND, 4, 18)),
+                pltpu.SemaphoreType.DMA((ND, 28)),
+                pltpu.SemaphoreType.DMA((ND, 20)),
                 pltpu.SemaphoreType.DMA((ND, 2)),
                 pltpu.SemaphoreType.DMA((ND, 2)),
             ],
@@ -457,7 +460,7 @@
             out_shape=(up, down, up, down, jax.ShapeDtypeStruct((TOK, DM), BF16)),
             in_specs=[vm_spec, vm_spec],
             out_specs=(any_spec,) * 5,
-            scratch_shapes=[pltpu.SemaphoreType.DMA((NQ * 8 + 1,))],
+            scratch_shapes=[pltpu.SemaphoreType.DMA((5,))],
             compiler_params=pltpu.CompilerParams(vmem_limit_bytes=2**20),
         )(grads, dx)
 

time: 139 us -> 135 us (0.971)
  Pallas kernels: 139 us -> 134 us
    pallas_call x1, Pallas kernels: 132 us -> 127 us  [per_device(): pl.pallas_call(kernel, out_shape=(pltpu.VMEM((NQ, 2, 4, 512, 128), F32),...]
where the time goes in v5:
time: 135 us; the launch traced here: 134 us
  Pallas kernels  134 us (99%)
    pallas_call x1, Pallas kernels, per_device(): pl.pallas_call(kernel, out_shape=(pltpu.VMEM((NQ, 2, 4, 512, 128), F32),...  127 us
    pallas_call x1, Pallas kernels, per_device(): pl.pallas_call(finish, out_shape=(up, down, up, down, jax.ShapeDtypeStruc...  6.44 us

profile of v5, /device:TPU:1, one launch (start us, length us, event | category | flops | bytes accessed | tf_op | source)
XLA Modules:
  0.0 134.4 jit_solution(9157233336381230862)
XLA Ops:
  0.6 127.1 %shard_map.101 = (f32[8,2,4,512,128]{4,3,2,1,0:T(8,128)S(1)}, bf16[2048,512]{1,0:T(8,128)(2,1)S(1)}) custom-call(bf16[2048,512]{1,0:T(8,128)(2,1)} %x_hbm.1, bf16[2048,512]{1,0:T(8,128)(2,1)} %g_hbm.1, bf16[512,2048]{1,0:T(8,128)(2,1)} %w1_hbm.1, bf16[2048,512]{1,0:T(8,128)(2,1)} %w2_hbm.1, bf16[512,2048]{1,0:T(8,128)(2,1)} %w3_hbm.1, bf16[2048,512]{1,0:T(8,128)(2,1)} %w4_hbm.1), custom_call_target="tpu_custom_call" | custom-call | flops 51539607552 | bytes 33554432 | tf_op jit(solution)/shard_map/pallas_call | solution.py:430
  127.8 6.4 %shard_map.102 = (f32[512,2048]{1,0:T(8,128)}, f32[2048,512]{1,0:T(8,128)}, f32[512,2048]{1,0:T(8,128)}, f32[2048,512]{1,0:T(8,128)}, bf16[2048,512]{1,0:T(8,128)(2,1)}) custom-call(f32[8,2,4,512,128]{4,3,2,1,0:T(8,128)S(1)} %get-tuple-element.7.gb, bf16[2048,512]{1,0:T(8,128)(2,1)S(1)} %get-tuple-element.8.dx), custom_call_target="tpu_custom_call" | custom-call | tf_op jit(solution)/shard_map/pallas_call | solution.py:458

commit v6 on v5

--- a/solution.py
+++ b/solution.py
@@ -66,30 +66,29 @@
     at = [[lax.rem(p + j, 4) for p in (cx, y, z)] for j in range(4)]
     dev = [[me + (at[j][d] - at[0][d]) * stride for d, stride in enumerate((2, 8, 32))] for j in range(4)]
 
-    loads = []
-    n = 0
-
-    def load(src, dst):
-        nonlocal n
-        cp = pltpu.make_async_copy(src, dst, in_sem.at[n])
-        cp.start()
-        n += 1
-        return cp
-
-    ld_x = load(x_hbm, xv)
-    ld_w1 = [load(w1_hbm.at[:, pl.ds(c * CB, CB)], w1.at[c]) for c in range(NB)]
-    ld_w2 = [load(w2_hbm.at[pl.ds(c * CB, CB), :], w2.at[c]) for c in range(NB)]
+    def load_blocks(n, hbm, vmem, by_rows):
+        for c in range(NB):
+            span = pl.ds(c * CB, CB)
+            src = hbm.at[span, :] if by_rows else hbm.at[:, span]
+            pltpu.make_async_copy(src, vmem.at[c], in_sem.at[n]).start()
+
+    def load_wait(n, hbm):
+        pltpu.make_async_copy(hbm, hbm, in_sem.at[n]).wait()
+
+    pltpu.make_async_copy(x_hbm, xv, in_sem.at[0]).start()
+    load_blocks(1, w1_hbm, w1, False)
+    load_blocks(2, w2_hbm, w2, True)
+
     barrier = pltpu.get_barrier_semaphore()
     peers = [partner] + [dev[j][d] for j in (1, 2, 3) for d in range(3)]
     for peer in peers:
         pl.semaphore_signal(barrier, inc=1, device_id=peer, device_id_type=LOGICAL)
 
-    ld_x.wait()
-    for cp in ld_w1 + ld_w2:
-        cp.wait()
-    ld_w3 = [load(w3_hbm.at[:, pl.ds(c * CB, CB)], w3.at[c]) for c in range(NB)]
-    ld_g = load(g_hbm, gv)
-    ld_w4 = [load(w4_hbm.at[pl.ds(c * CB, CB), :], w4.at[c]) for c in range(NB)]
+    for n, hbm in enumerate((x_hbm, w1_hbm, w2_hbm)):
+        load_wait(n, hbm)
+    load_blocks(3, w3_hbm, w3, False)
+    pltpu.make_async_copy(g_hbm, gv, in_sem.at[4]).start()
+    load_blocks(5, w4_hbm, w4, True)
 
     def fwd1(t, carry):
         rows = pl.ds(pl.multiple_of(t * TT, TT), TT)
@@ -103,8 +102,8 @@
         return carry
 
     lax.fori_loop(0, NT, fwd1, 0)
-    for cp in ld_w3 + [ld_g] + ld_w4:
-        cp.wait()
+    for n, hbm in enumerate((w3_hbm, g_hbm, w4_hbm)):
+        load_wait(n + 3, hbm)
     pl.semaphore_wait(barrier, len(peers))
 
     class Chunk:
@@ -445,7 +444,7 @@
                 pltpu.VMEM((2, TOK, CB), BF16),
                 pltpu.VMEM((ND, 4, 512, 128), F32),
                 pltpu.VMEM((SL, 4, 504, 128), F32),
-                pltpu.SemaphoreType.DMA((18,)),
+                pltpu.SemaphoreType.DMA((6,)),
                 pltpu.SemaphoreType.DMA((ND, 28)),
                 pltpu.SemaphoreType.DMA((ND, 20)),
                 pltpu.SemaphoreType.DMA((ND, 2)),

time: 135 us -> 134 us (level)
  no operation moved by 1% of the time
where the time goes in v6:
time: 134 us
  Pallas kernels  133 us (99%)
    pallas_call x1, Pallas kernels, per_device(): pl.pallas_call(kernel, out_shape=(pltpu.VMEM((NQ, 2, 4, 512, 128), F32),...  127 us
    pallas_call x1, Pallas kernels, per_device(): pl.pallas_call(finish, out_shape=(up, down, up, down, jax.ShapeDtypeStruc...  6.44 us

profile of v6, /device:TPU:1, one launch (start us, length us, event | category | flops | bytes accessed | tf_op | source)
XLA Modules:
  0.0 134.3 jit_solution(7828690852424935609)
XLA Ops:
  0.6 127.0 %shard_map.101 = (f32[8,2,4,512,128]{4,3,2,1,0:T(8,128)S(1)}, bf16[2048,512]{1,0:T(8,128)(2,1)S(1)}) custom-call(bf16[2048,512]{1,0:T(8,128)(2,1)} %x_hbm.1, bf16[2048,512]{1,0:T(8,128)(2,1)} %g_hbm.1, bf16[512,2048]{1,0:T(8,128)(2,1)} %w1_hbm.1, bf16[2048,512]{1,0:T(8,128)(2,1)} %w2_hbm.1, bf16[512,2048]{1,0:T(8,128)(2,1)} %w3_hbm.1, bf16[2048,512]{1,0:T(8,128)(2,1)} %w4_hbm.1), custom_call_target="tpu_custom_call" | custom-call | flops 51539607552 | bytes 33554432 | tf_op jit(solution)/shard_map/pallas_call | solution.py:429
  127.7 6.4 %shard_map.102 = (f32[512,2048]{1,0:T(8,128)}, f32[2048,512]{1,0:T(8,128)}, f32[512,2048]{1,0:T(8,128)}, f32[2048,512]{1,0:T(8,128)}, bf16[2048,512]{1,0:T(8,128)(2,1)}) custom-call(f32[8,2,4,512,128]{4,3,2,1,0:T(8,128)S(1)} %get-tuple-element.7.gb, bf16[2048,512]{1,0:T(8,128)(2,1)S(1)} %get-tuple-element.8.dx), custom_call_target="tpu_custom_call" | custom-call | tf_op jit(solution)/shard_map/pallas_call | solution.py:457
